TPU v7x, 32 devices: a whole 2x2x4 slice. The times are simulated.
32 devices in a mesh: ctx: 4 (over z), fsdp: 8 (over y, x, core).
Axes of the slice: x: 2, y: 2, z: 4, core: 2. Of those that a mesh axis runs over, the one named last changes fastest.
Arguments:
- inputs: bfloat16 [8, 1024, 896], P('fsdp', 'ctx'), may hold values from -60 to 60
- positions: int32 [8, 1024], P('fsdp', 'ctx'), may hold values from 0 to 1023, as said below
- cotangent: bfloat16 [8, 1024, 896], P('fsdp', 'ctx'), may hold values from -6 to 6
- norm_one: bfloat16 [1, 896], P(None, 'fsdp'), may hold values from 0.5 to 1.5
- w_query: bfloat16 [1, 896, 896], P(None, 'fsdp'), may hold values from -0.1875 to 0.1875
- b_query: bfloat16 [1, 896], P(None, 'fsdp'), may hold values from -2 to 2
- key_projection: bfloat16 [1, 896, 128], P(None, 'fsdp'), may hold values from -0.1875 to 0.1875
- b_key: bfloat16 [1, 128], P(None, 'fsdp'), may hold values from -2 to 2
- value_projection: bfloat16 [1, 896, 128], P(None, 'fsdp'), may hold values from -0.1875 to 0.1875
- value_bias: bfloat16 [1, 128], P(None, 'fsdp'), may hold values from -3 to 3
- w_out: bfloat16 [1, 896, 896], P(None, 'fsdp'), may hold values from -0.75 to 0.75
- norm_two: bfloat16 [1, 896], P(None, 'fsdp'), may hold values from 0.5 to 1.5
- w_gate: bfloat16 [1, 896, 4864], P(None, 'fsdp'), may hold values from -0.1875 to 0.1875
- w_up: bfloat16 [1, 896, 4864], P(None, 'fsdp'), may hold values from -0.1875 to 0.1875
- w_down: bfloat16 [1, 4864, 896], P(None, 'fsdp'), may hold values from -0.078125 to 0.078125
Outputs:
- output: float32 [8, 1024, 896], P('fsdp', 'ctx')
- grad_inputs: float32 [8, 1024, 896], P('fsdp', 'ctx')
- grad_norm_one: float32 [1, 896], P(None, 'fsdp')
- grad_w_query: float32 [1, 896, 896], P(None, 'fsdp')
- grad_b_query: float32 [1, 896], P(None, 'fsdp')
- grad_w_key: float32 [1, 896, 128], P(None, 'fsdp')
- grad_b_key: float32 [1, 128], P(None, 'fsdp')
- grad_w_value: float32 [1, 896, 128], P(None, 'fsdp')
- grad_b_value: float32 [1, 128], P(None, 'fsdp')
- grad_w_out: float32 [1, 896, 896], P(None, 'fsdp')
- grad_norm_two: float32 [1, 896], P(None, 'fsdp')
- grad_w_gate: float32 [1, 896, 4864], P(None, 'fsdp')
- grad_w_up: float32 [1, 896, 4864], P(None, 'fsdp')
- grad_w_down: float32 [1, 4864, 896], P(None, 'fsdp')
Inputs may be any that keep to these rules, and one draw needn't show every extreme that they name: In each sequence every position 0 to 1023 stands in exactly one slot; each aligned block of 256 slots (one device's) holds two whole blocks of 128 consecutive positions, rising within a block: block b and block 7 - b.
All inputs are finite; a program needn't handle non-finite values.
Results may differ from a plain program's by a relative error of at most 0.02.
Values may be sent and summed in bfloat16 or wider, within the bound.
A program may use at most 192 MiB of HBM per device.

v0:
```python
import math

import jax
import jax.numpy as jnp
from jax import lax
from jax.sharding import PartitionSpec as P

QUERY_HEADS = 14
KEY_VALUE_HEADS = 2
HEAD_SIZE = 64
DECODER_LAYERS = 1


rope_base = 1000000.0
epsilon = 1e-06
negative = -1e30


def angles(places, head_width):
    half_width = head_width // 2
    inverse = jnp.exp(
        jnp.arange(half_width, dtype=jnp.float32) * (-2.0 * math.log(rope_base) / head_width)
    )
    turned = places.astype(jnp.float32)[:, None] * inverse[None, :]
    return (jnp.cos(turned)[:, None, :], jnp.sin(turned)[:, None, :])


def apply_rotation(value_entries, cosine_table, sine_table):
    half_width = value_entries.shape[-1] // 2
    first_half = value_entries[..., :half_width]
    second_half = value_entries[..., half_width:]
    return jnp.concatenate(
        [
            first_half * cosine_table - second_half * sine_table,
            second_half * cosine_table + first_half * sine_table,
        ],
        axis=-1,
    )


def norm_rows(hidden, gain):
    scale_row = lax.rsqrt(jnp.mean(hidden * hidden, axis=-1, keepdims=True) + epsilon)
    return (scale_row, (hidden * scale_row * gain.astype(jnp.float32)).astype(jnp.bfloat16))


def norm_back(hidden, scale_row, gain, grad_normed):
    weighted = gain.astype(jnp.float32) * grad_normed
    grad_gain = jnp.sum(grad_normed * hidden * scale_row, axis=0)
    inner_mean = jnp.mean(weighted * hidden, axis=-1, keepdims=True)
    return (
        grad_gain,
        scale_row * weighted - hidden * (scale_row * scale_row * scale_row) * inner_mean,
    )


def scores_of(query_rows, key_block, places, block_places):
    raw_scores = jnp.einsum(
        "tgjd,ugd->gjtu", query_rows, key_block, preferred_element_type=jnp.float32
    ) * (1.0 / math.sqrt(HEAD_SIZE))
    return jnp.where(block_places[None, :] <= places[:, None], raw_scores, negative)


def split_blocks(gathered_keys, gathered_values, key_places):
    total_length = gathered_keys.shape[0]
    block_length = min(512, total_length)
    number_of_blocks = total_length // block_length
    key_block_list = gathered_keys.reshape(
        number_of_blocks, block_length, KEY_VALUE_HEADS, HEAD_SIZE
    )
    value_block_list = gathered_values.reshape(
        number_of_blocks, block_length, KEY_VALUE_HEADS, HEAD_SIZE
    )
    place_blocks = key_places.reshape(number_of_blocks, block_length)
    return (key_block_list, value_block_list, place_blocks)


def attend(query_rows, gathered_keys, gathered_values, places, key_places):
    number_of_rows = query_rows.shape[0]
    heads_per_group = QUERY_HEADS // KEY_VALUE_HEADS
    key_block_list, value_block_list, place_blocks = split_blocks(
        gathered_keys, gathered_values, key_places
    )
    statistic_shape = (KEY_VALUE_HEADS, heads_per_group, number_of_rows)

    def measure(carry, block_item):
        top_score, totals = carry
        key_block, block_places = block_item
        block_scores = scores_of(query_rows, key_block, places, block_places)
        fresh_top = jnp.maximum(top_score, jnp.max(block_scores, axis=-1))
        totals = totals * jnp.exp(top_score - fresh_top) + jnp.sum(
            jnp.exp(block_scores - fresh_top[..., None]), axis=-1
        )
        return ((fresh_top, totals), None)

    start_carry = (
        jnp.full(statistic_shape, negative, jnp.float32),
        jnp.zeros(statistic_shape, jnp.float32),
    )
    (top_score, totals), unused = lax.scan(measure, start_carry, (key_block_list, place_blocks))
    log_total = top_score + jnp.log(totals)

    def collect(running, block_item):
        key_block, value_block, block_places = block_item
        attn_probs = jnp.exp(
            scores_of(query_rows, key_block, places, block_places) - log_total[..., None]
        ).astype(jnp.bfloat16)
        return (
            running
            + jnp.einsum(
                "gjtu,ugd->tgjd", attn_probs, value_block, preferred_element_type=jnp.float32
            ),
            None,
        )

    mixture, unused = lax.scan(
        collect,
        jnp.zeros((number_of_rows, KEY_VALUE_HEADS, heads_per_group, HEAD_SIZE), jnp.float32),
        (key_block_list, value_block_list, place_blocks),
    )
    return (mixture, log_total)


def attend_back(
    query_rows, gathered_keys, gathered_values, places, key_places, log_total, grad_mixture
):
    number_of_rows = query_rows.shape[0]
    total_length = gathered_keys.shape[0]
    heads_per_group = QUERY_HEADS // KEY_VALUE_HEADS
    key_block_list, value_block_list, place_blocks = split_blocks(
        gathered_keys, gathered_values, key_places
    )

    def first_pass(delta_row, block_item):
        key_block, value_block, block_places = block_item
        attn_probs = jnp.exp(
            scores_of(query_rows, key_block, places, block_places) - log_total[..., None]
        )
        grad_probs = jnp.einsum(
            "tgjd,ugd->gjtu", grad_mixture, value_block, preferred_element_type=jnp.float32
        )
        return (delta_row + jnp.sum(attn_probs * grad_probs, axis=-1), None)

    delta_row, unused = lax.scan(
        first_pass,
        jnp.zeros((KEY_VALUE_HEADS, heads_per_group, number_of_rows), jnp.float32),
        (key_block_list, value_block_list, place_blocks),
    )

    def second_pass(grad_queries, block_item):
        key_block, value_block, block_places = block_item
        attn_probs = jnp.exp(
            scores_of(query_rows, key_block, places, block_places) - log_total[..., None]
        )
        grad_probs = jnp.einsum(
            "tgjd,ugd->gjtu", grad_mixture, value_block, preferred_element_type=jnp.float32
        )
        grad_scores = (attn_probs * (grad_probs - delta_row[..., None])).astype(jnp.bfloat16)
        grad_queries = grad_queries + jnp.einsum(
            "gjtu,ugd->tgjd", grad_scores, key_block, preferred_element_type=jnp.float32
        )
        grad_key_block = jnp.einsum(
            "gjtu,tgjd->ugd", grad_scores, query_rows, preferred_element_type=jnp.float32
        )
        grad_value_block = jnp.einsum(
            "gjtu,tgjd->ugd",
            attn_probs.astype(jnp.bfloat16),
            grad_mixture,
            preferred_element_type=jnp.float32,
        )
        return (grad_queries, (grad_key_block, grad_value_block))

    grad_queries, (key_gradient, value_gradient) = lax.scan(
        second_pass,
        jnp.zeros((number_of_rows, KEY_VALUE_HEADS, heads_per_group, HEAD_SIZE), jnp.float32),
        (key_block_list, value_block_list, place_blocks),
    )
    score_scale = 1.0 / math.sqrt(HEAD_SIZE)
    return (
        grad_queries * score_scale,
        key_gradient.reshape(total_length, KEY_VALUE_HEADS * HEAD_SIZE) * score_scale,
        value_gradient.reshape(total_length, KEY_VALUE_HEADS * HEAD_SIZE),
    )


def layer_forward(hidden, weights, places, key_places, cosine_table, sine_table):
    (
        gain_one,
        w_query,
        b_query,
        key_projection,
        b_key,
        value_projection,
        value_bias,
        w_out,
        gain_two,
        w_gate,
        w_up,
        w_down,
    ) = weights
    number_of_rows = hidden.shape[0]
    heads_per_group = QUERY_HEADS // KEY_VALUE_HEADS
    scale_one, normed = norm_rows(hidden, gain_one)
    query_rows = jnp.dot(normed, w_query, preferred_element_type=jnp.float32) + b_query.astype(
        jnp.float32
    )
    key_row_slice = jnp.dot(
        normed, key_projection, preferred_element_type=jnp.float32
    ) + b_key.astype(jnp.float32)
    value_row_slice = jnp.dot(
        normed, value_projection, preferred_element_type=jnp.float32
    ) + value_bias.astype(jnp.float32)
    query_rows = (
        apply_rotation(
            query_rows.reshape(number_of_rows, QUERY_HEADS, HEAD_SIZE), cosine_table, sine_table
        )
        .astype(jnp.bfloat16)
        .reshape(number_of_rows, KEY_VALUE_HEADS, heads_per_group, HEAD_SIZE)
    )
    key_row_slice = (
        apply_rotation(
            key_row_slice.reshape(number_of_rows, KEY_VALUE_HEADS, HEAD_SIZE),
            cosine_table,
            sine_table,
        )
        .astype(jnp.bfloat16)
        .reshape(number_of_rows, KEY_VALUE_HEADS * HEAD_SIZE)
    )
    value_row_slice = value_row_slice.astype(jnp.bfloat16)
    gathered_keys, gathered_values = (
        lax.all_gather(key_row_slice, "ctx", axis=0, tiled=True),
        lax.all_gather(value_row_slice, "ctx", axis=0, tiled=True),
    )
    mixture, log_total = attend(query_rows, gathered_keys, gathered_values, places, key_places)
    mixture = mixture.reshape(number_of_rows, QUERY_HEADS * HEAD_SIZE).astype(jnp.bfloat16)
    middle = hidden + jnp.dot(mixture, w_out, preferred_element_type=jnp.float32)
    scale_two, normed_two = norm_rows(middle, gain_two)
    gate_act = jnp.dot(normed_two, w_gate, preferred_element_type=jnp.float32)
    up_act = jnp.dot(normed_two, w_up, preferred_element_type=jnp.float32)
    inner_act = (jax.nn.silu(gate_act) * up_act).astype(jnp.bfloat16)
    output = middle + jnp.dot(inner_act, w_down, preferred_element_type=jnp.float32)
    record = (
        hidden,
        scale_one,
        normed,
        query_rows,
        gathered_keys,
        gathered_values,
        log_total,
        mixture,
        middle,
        scale_two,
        normed_two,
        gate_act,
        up_act,
        inner_act,
    )
    return (output, record)


def layer_backward(grad_out, weights, record, places, key_places, cosine_table, sine_table):
    (
        gain_one,
        w_query,
        b_query,
        key_projection,
        b_key,
        value_projection,
        value_bias,
        w_out,
        gain_two,
        w_gate,
        w_up,
        w_down,
    ) = weights
    (
        hidden,
        scale_one,
        normed,
        query_rows,
        gathered_keys,
        gathered_values,
        log_total,
        mixture,
        middle,
        scale_two,
        normed_two,
        gate_act,
        up_act,
        inner_act,
    ) = record
    number_of_rows = hidden.shape[0]
    heads_per_group = QUERY_HEADS // KEY_VALUE_HEADS
    grad_branch = grad_out.astype(jnp.bfloat16)
    grad_down = jnp.einsum("tf,td->fd", inner_act, grad_branch, preferred_element_type=jnp.float32)
    grad_inner = jnp.einsum("td,fd->tf", grad_branch, w_down, preferred_element_type=jnp.float32)
    sigmoid_gate = jax.nn.sigmoid(gate_act)
    grad_gate = (
        grad_inner * up_act * sigmoid_gate * (1.0 + gate_act * (1.0 - sigmoid_gate))
    ).astype(jnp.bfloat16)
    grad_up = (grad_inner * (gate_act * sigmoid_gate)).astype(jnp.bfloat16)
    grad_gate_w = jnp.einsum("tc,tf->cf", normed_two, grad_gate, preferred_element_type=jnp.float32)
    grad_up_w = jnp.einsum("tc,tf->cf", normed_two, grad_up, preferred_element_type=jnp.float32)
    grad_normed_two = jnp.einsum(
        "tf,cf->tc", grad_gate, w_gate, preferred_element_type=jnp.float32
    ) + jnp.einsum("tf,cf->tc", grad_up, w_up, preferred_element_type=jnp.float32)
    grad_gain_two, grad_middle = norm_back(middle, scale_two, gain_two, grad_normed_two)
    grad_middle = grad_out + grad_middle
    grad_attn = grad_middle.astype(jnp.bfloat16)
    grad_out_w = jnp.einsum("te,td->ed", mixture, grad_attn, preferred_element_type=jnp.float32)
    grad_mixture = (
        jnp.einsum("td,ed->te", grad_attn, w_out, preferred_element_type=jnp.float32)
        .astype(jnp.bfloat16)
        .reshape(number_of_rows, KEY_VALUE_HEADS, heads_per_group, HEAD_SIZE)
    )
    grad_queries, grad_key_all, grad_value_all = attend_back(
        query_rows, gathered_keys, gathered_values, places, key_places, log_total, grad_mixture
    )
    key_gradient, value_gradient = (
        lax.psum_scatter(grad_key_all, "ctx", scatter_dimension=0, tiled=True),
        lax.psum_scatter(grad_value_all, "ctx", scatter_dimension=0, tiled=True),
    )
    grad_queries = (
        apply_rotation(
            grad_queries.reshape(number_of_rows, QUERY_HEADS, HEAD_SIZE), cosine_table, -sine_table
        )
        .astype(jnp.bfloat16)
        .reshape(number_of_rows, QUERY_HEADS * HEAD_SIZE)
    )
    key_gradient = (
        apply_rotation(
            key_gradient.reshape(number_of_rows, KEY_VALUE_HEADS, HEAD_SIZE),
            cosine_table,
            -sine_table,
        )
        .astype(jnp.bfloat16)
        .reshape(number_of_rows, KEY_VALUE_HEADS * HEAD_SIZE)
    )
    value_gradient = value_gradient.astype(jnp.bfloat16)
    grad_query_w = jnp.einsum("tc,te->ce", normed, grad_queries, preferred_element_type=jnp.float32)
    grad_key_w = jnp.einsum("tc,te->ce", normed, key_gradient, preferred_element_type=jnp.float32)
    grad_value_w = jnp.einsum(
        "tc,te->ce", normed, value_gradient, preferred_element_type=jnp.float32
    )
    grad_query_b = jnp.sum(grad_queries.astype(jnp.float32), axis=0)
    grad_key_b = jnp.sum(key_gradient.astype(jnp.float32), axis=0)
    grad_value_b = jnp.sum(value_gradient.astype(jnp.float32), axis=0)
    grad_normed = jnp.einsum("te,ce->tc", grad_queries, w_query, preferred_element_type=jnp.float32)
    grad_normed = grad_normed + jnp.einsum(
        "te,ce->tc", key_gradient, key_projection, preferred_element_type=jnp.float32
    )
    grad_normed = grad_normed + jnp.einsum(
        "te,ce->tc", value_gradient, value_projection, preferred_element_type=jnp.float32
    )
    grad_gain_one, grad_hidden = norm_back(hidden, scale_one, gain_one, grad_normed)
    grad_terms = (
        grad_gain_one,
        grad_query_w,
        grad_query_b,
        grad_key_w,
        grad_key_b,
        grad_value_w,
        grad_value_b,
        grad_out_w,
        grad_gain_two,
        grad_gate_w,
        grad_up_w,
        grad_down,
    )
    return (grad_middle + grad_hidden, grad_terms)


def shards(
    inputs,
    positions,
    cotangent,
    norm_one,
    w_query,
    b_query,
    key_projection,
    b_key,
    value_projection,
    value_bias,
    w_out,
    norm_two,
    w_gate,
    w_up,
    w_down,
):
    places = positions[0]
    key_places = lax.all_gather(places, "ctx", axis=0, tiled=True)
    cosine_table, sine_table = angles(places, HEAD_SIZE)
    hidden = inputs[0].astype(jnp.float32)
    gathered_list = []
    layer_index = 0
    gathered = (
        lax.all_gather(norm_one[layer_index], "fsdp", axis=0, tiled=True),
        lax.all_gather(w_query[layer_index], "fsdp", axis=0, tiled=True),
        lax.all_gather(b_query[layer_index], "fsdp", axis=0, tiled=True),
        lax.all_gather(key_projection[layer_index], "fsdp", axis=0, tiled=True),
        lax.all_gather(b_key[layer_index], "fsdp", axis=0, tiled=True),
        lax.all_gather(value_projection[layer_index], "fsdp", axis=0, tiled=True),
        lax.all_gather(value_bias[layer_index], "fsdp", axis=0, tiled=True),
        lax.all_gather(w_out[layer_index], "fsdp", axis=0, tiled=True),
        lax.all_gather(norm_two[layer_index], "fsdp", axis=0, tiled=True),
        lax.all_gather(w_gate[layer_index], "fsdp", axis=0, tiled=True),
        lax.all_gather(w_up[layer_index], "fsdp", axis=0, tiled=True),
        lax.all_gather(w_down[layer_index], "fsdp", axis=0, tiled=True),
    )
    hidden, record = layer_forward(hidden, gathered, places, key_places, cosine_table, sine_table)
    records = [record]
    gathered_list.append(gathered)
    grad_out = cotangent[0].astype(jnp.float32)
    shares = []
    for layer_index in reversed(range(DECODER_LAYERS)):
        weights = (
            lax.all_gather(norm_one[layer_index], "fsdp", axis=0, tiled=True),
            lax.all_gather(w_query[layer_index], "fsdp", axis=0, tiled=True),
            lax.all_gather(b_query[layer_index], "fsdp", axis=0, tiled=True),
            lax.all_gather(key_projection[layer_index], "fsdp", axis=0, tiled=True),
            lax.all_gather(b_key[layer_index], "fsdp", axis=0, tiled=True),
            lax.all_gather(value_projection[layer_index], "fsdp", axis=0, tiled=True),
            lax.all_gather(value_bias[layer_index], "fsdp", axis=0, tiled=True),
            lax.all_gather(w_out[layer_index], "fsdp", axis=0, tiled=True),
            lax.all_gather(norm_two[layer_index], "fsdp", axis=0, tiled=True),
            lax.all_gather(w_gate[layer_index], "fsdp", axis=0, tiled=True),
            lax.all_gather(w_up[layer_index], "fsdp", axis=0, tiled=True),
            lax.all_gather(w_down[layer_index], "fsdp", axis=0, tiled=True),
        )
        grad_out, grad_terms = layer_backward(
            grad_out, weights, records[layer_index], places, key_places, cosine_table, sine_table
        )
        ffn_share = (
            lax.psum_scatter(grad_terms[8], "fsdp", scatter_dimension=0, tiled=True),
            lax.psum_scatter(grad_terms[9], "fsdp", scatter_dimension=0, tiled=True),
            lax.psum_scatter(grad_terms[10], "fsdp", scatter_dimension=0, tiled=True),
            lax.psum_scatter(grad_terms[11], "fsdp", scatter_dimension=0, tiled=True),
        )
        attn_share = (
            lax.psum_scatter(grad_terms[0], "fsdp", scatter_dimension=0, tiled=True),
            lax.psum_scatter(grad_terms[1], "fsdp", scatter_dimension=0, tiled=True),
            lax.psum_scatter(grad_terms[2], "fsdp", scatter_dimension=0, tiled=True),
            lax.psum_scatter(grad_terms[3], "fsdp", scatter_dimension=0, tiled=True),
            lax.psum_scatter(grad_terms[4], "fsdp", scatter_dimension=0, tiled=True),
            lax.psum_scatter(grad_terms[5], "fsdp", scatter_dimension=0, tiled=True),
            lax.psum_scatter(grad_terms[6], "fsdp", scatter_dimension=0, tiled=True),
            lax.psum_scatter(grad_terms[7], "fsdp", scatter_dimension=0, tiled=True),
        )
        layer_share = tuple(attn_share) + tuple(ffn_share)
        layer_share = lax.psum(
            (
                layer_share[0],
                layer_share[1],
                layer_share[2],
                layer_share[3],
                layer_share[4],
                layer_share[5],
                layer_share[6],
                layer_share[7],
                layer_share[8],
                layer_share[9],
                layer_share[10],
                layer_share[11],
            ),
            "ctx",
        )
        shares.insert(0, layer_share)
    stacked = [jnp.stack([shares[0][kind_index]]) for kind_index in range(12)]
    return (
        hidden[None],
        grad_out[None],
        stacked[0],
        stacked[1],
        stacked[2],
        stacked[3],
        stacked[4],
        stacked[5],
        stacked[6],
        stacked[7],
        stacked[8],
        stacked[9],
        stacked[10],
        stacked[11],
    )


def solution(mesh):
    return jax.shard_map(
        shards,
        mesh=mesh,
        in_specs=(
            P("fsdp", "ctx", None),
            P("fsdp", "ctx"),
            P("fsdp", "ctx", None),
            P(None, "fsdp"),
            P(None, "fsdp", None),
            P(None, "fsdp"),
            P(None, "fsdp", None),
            P(None, "fsdp"),
            P(None, "fsdp", None),
            P(None, "fsdp"),
            P(None, "fsdp", None),
            P(None, "fsdp"),
            P(None, "fsdp", None),
            P(None, "fsdp", None),
            P(None, "fsdp", None),
        ),
        out_specs=(
            P("fsdp", "ctx", None),
            P("fsdp", "ctx", None),
            P(None, "fsdp"),
            P(None, "fsdp", None),
            P(None, "fsdp"),
            P(None, "fsdp", None),
            P(None, "fsdp"),
            P(None, "fsdp", None),
            P(None, "fsdp"),
            P(None, "fsdp", None),
            P(None, "fsdp"),
            P(None, "fsdp", None),
            P(None, "fsdp", None),
            P(None, "fsdp", None),
        ),
        check_vma=False,
    )
```

profile of v0, /device:TPU:0, one launch (start us, length us, event | category | flops | bytes accessed | tf_op | source)
XLA Modules:
  0.0 1228.1 jit_solution(17553503487937079798)
XLA Ops:
  17.6 15.5 %all-reduce.13 = (bf16[128]{0:T(256)(128)(2,1)S(1)}, bf16[896]{0:T(1024)(128)(2,1)S(1)}, bf16[128]{0:T(256)(128)(2,1)S(1)}, bf16[896]{0:T(1024)(128)(2,1)S(1)}, bf16[896]{0:T(1024)(128)(2,1)S(1)}) all-reduce(bf16[128]{0:T(256)(128)(2,1)S(1)} %dynamic-update-slice.1, ...), channel_id=4, replica_groups=mesh['ctx'=4,'fsdp'=8] {'fsdp'}, use_global_device_ids=true, to_apply=%add.1 | all-reduce | flops 2944 | bytes 11776
  33.2 8.6 all-gather.1
  43.6 1.4 fusion.115
  45.0 14.0 %all_gather.57 = bf16[1024,128]{1,0:T(8,128)(2,1)S(1)} all-gather(bf16[256,128]{1,0:T(8,128)(2,1)S(1)} %fusion.115), channel_id=1, replica_groups=mesh['ctx'=4,'fsdp'=8] {'ctx'}, dimensions={0}, use_global_device_ids=true | all-gather | bytes 327680 | tf_op jit(solution)/shard_map/all_gather | solution.py:231
  60.3 11.6 all-gather.3
  73.1 10.0 all-gather.4
  84.3 14.4 %all_gather.61 = bf16[1024,128]{0,1:T(8,128)(2,1)S(1)} all-gather(bf16[256,128]{0,1:T(8,128)(2,1)S(1)} %bitcast.415), channel_id=1, replica_groups=mesh['ctx'=4,'fsdp'=8] {'ctx'}, dimensions={0}, use_global_device_ids=true | all-gather | bytes 327680 | tf_op jit(solution)/shard_map/all_gather | solution.py:230
  99.0 3.1 fusion.86
  102.1 1.5 copy.67
  103.8 18.1 %while.50 = (s32[]{:T(128)}, f32[2,7,256]{2,1,0:T(8,128)S(1)}, f32[2,7,256]{2,1,0:T(8,128)S(1)}, s32[2,512]{1,0:T(2,128)S(1)}, s32[1,256]{1,0:T(1,128)S(1)}, /*i...) while((s32[]{:T(128)}, f32[2,7,256]{2,1,0:T(8,128)S(1)}, ...), condition=%wide.region_4.5_spmd.clone, body=%wide.region_1.4_spmd.clone.sunk | while | flops 247875072 | bytes 15856760 | solution.py:99
  104.2 4.1 fusion.212
  108.4 4.6 exponential_reduce_fusion.2
  113.1 4.1 fusion.212
  117.2 4.6 exponential_reduce_fusion.2
  121.9 9.0 while.51
  122.1 4.2 fusion.218
  126.4 4.5 fusion.218
  130.9 1.4 convert_element_type.144
  132.3 2.6 multiply_reduce_fusion.2
  136.0 10.0 fusion.65
  146.0 35.2 %all-gather.25.cloned.1.call-done = bf16[1,896,4864]{2,1,0:T(8,128)(2,1)} async-done(((bf16[1,112,4864]{2,1,0:T(8,128)(2,1)}), bf16[1,896,4864]{2,1,0:T(8,128)(2,1)}) %all-gather.25.cloned.1.call-update) | async-done | bytes 8716304 | tf_op jit(solution)/shard_map/all_gather | solution.py:406
  181.2 7.9 fusion.71
  189.2 49.5 %all-gather.23.cloned.1.call-done = bf16[1,896,4864]{2,1,0:T(8,128)(2,1)} async-done(((bf16[1,112,4864]{2,1,0:T(8,128)(2,1)}), bf16[1,896,4864]{2,1,0:T(8,128)(2,1)}) %all-gather.23.cloned.1.call-update) | async-done | bytes 8716304 | tf_op jit(solution)/shard_map/all_gather | solution.py:405
  238.7 10.8 multiply_convert_fusion.1
  249.5 2.8 fusion.69
  252.3 6.5 multiply_reduce_fusion
  260.9 8.7 while.52
  262.2 3.0 fusion.224
  266.6 3.0 fusion.224
  269.6 45.0 %while.53 = (s32[]{:T(128)}, f32[256,2,7,64]{0,3,2,1:T(8,128)S(1)}, f32[2,512,2,64]{1,3,2,0:T(8,128)}, f32[2,512,2,64]{1,0,3,2:T(2,128)}, bf16[2,512,2,64]{1,3,2...) while((s32[]{:T(128)}, f32[256,2,7,64]{0,3,2,1:T(8,128)S(1)}, ...), condition=%wide.region_13.14_spmd.clone, body=%wide.region_12.13_spmd.clone.sunk | while | flops 1193345024 | bytes 91014488 | solution.py:172
  271.2 4.8 fusion.236
  276.0 3.0 fusion.237
  281.3 4.9 fusion.239
  286.5 5.8 dynamic_update_slice.13
  293.6 4.8 fusion.236
  298.4 3.0 fusion.237
  303.7 4.9 fusion.239
  308.9 5.8 dynamic_update_slice.13
  317.1 1.9 copy.105
  319.1 19.9 %reduce-scatter.10.cloned.1.call-done = f32[256,128]{0,1:T(8,128)} async-done(((f32[1024,128]{0,1:T(8,128)}), f32[256,128]{0,1:T(8,128)}) %reduce-scatter.10.cloned.1.call-update) | async-done | bytes 131088 | tf_op jit(solution)/shard_map/reduce_scatter | solution.py:319
  341.4 20.6 %reduce-scatter.12.cloned.1.call-done = f32[256,128]{0,1:T(8,128)} async-done(((f32[1024,128]{0,1:T(8,128)}), f32[256,128]{0,1:T(8,128)}) %reduce-scatter.12.cloned.1.call-update) | async-done | bytes 131088 | tf_op jit(solution)/shard_map/reduce_scatter | solution.py:320
  362.0 2.1 fusion.146
  364.6 2.6 fusion.143
  367.2 2.3 fusion.138
  369.6 10.2 fusion.154
  380.1 10.1 fusion.155
  391.3 10.5 fusion.129
  404.2 3.2 fusion.125
  407.4 22.6 %all-reduce.10 = (f32[896]{0:T(1024)S(1)}, f32[896]{0:T(1024)S(1)}, f32[128]{0:T(128)S(1)}, f32[128]{0:T(128)S(1)}, f32[896]{0:T(1024)S(1)}) all-reduce(f32[896]{0:T(1024)S(1)} %get-tuple-element.435, f32[896]{0:T(1024)S(1)} %reduce_sum.109, f32[128]{0:T(128)S(1)} %reduce_sum.111, ...), channel_id=17, replica_groups=mesh['ctx'=4,'fsdp'=8] {'fsdp'}, use_global_device_ids=true, to_apply=%region_18.19.clone | all-reduce | flops 2944 | bytes 23552
  431.7 3.9 reduce-scatter.18.cloned.1.call-done
  435.8 49.7 %reduce-scatter.14.cloned.1.call-done = f32[112,896]{1,0:T(8,128)} async-done(((f32[896,896]{1,0:T(8,128)}), f32[112,896]{1,0:T(8,128)}) %reduce-scatter.14.cloned.1.call-update) | async-done | bytes 401424 | tf_op jit(solution)/shard_map/reduce_scatter | solution.py:440
  485.4 49.9 %reduce-scatter.20.cloned.1.call-done = f32[112,896]{1,0:T(8,128)} async-done(((f32[896,896]{1,0:T(8,128)}), f32[112,896]{1,0:T(8,128)}) %reduce-scatter.20.cloned.1.call-update) | async-done | bytes 401424 | tf_op jit(solution)/shard_map/reduce_scatter | solution.py:446
  535.3 123.0 %reduce-scatter.22.cloned.1.call-done = f32[112,4864]{1,0:T(8,128)} async-done(((f32[896,4864]{1,0:T(8,128)}), f32[112,4864]{1,0:T(8,128)}) %reduce-scatter.22.cloned.1.call-update) | async-done | bytes 2179088 | tf_op jit(solution)/shard_map/reduce_scatter | solution.py:434
  658.3 123.2 %reduce-scatter.24.cloned.1.call-done = f32[112,4864]{1,0:T(8,128)} async-done(((f32[896,4864]{1,0:T(8,128)}), f32[112,4864]{1,0:T(8,128)}) %reduce-scatter.24.cloned.1.call-update) | async-done | bytes 2179088 | tf_op jit(solution)/shard_map/reduce_scatter | solution.py:435
  781.5 123.0 %reduce-scatter.26.cloned.1.call-done = f32[608,896]{1,0:T(8,128)} async-done(((f32[4864,896]{1,0:T(8,128)}), f32[608,896]{1,0:T(8,128)}) %reduce-scatter.26.cloned.1.call-update) | async-done | bytes 2179088 | tf_op jit(solution)/shard_map/reduce_scatter | solution.py:436
  904.6 8.0 fusion.104
  913.8 29.8 %all-reduce.17.cloned.1.call-done = (f32[1,112]{1,0:T(1,128)}, f32[1,112]{1,0:T(1,128)}, f32[1,112,128]{2,1,0:T(8,128)}, f32[1,16]{1,0:T(1,128)}, f32[1,112,128]...) async-done(((f32[1,112]{1,0:T(1,128)}, f32[1,112]{1,0:T(1,128)}, f32[1,112,128]{2,1,0:T(8,128)}, f32[1,16]{1,0:T(1,128)}, f32[1,112,128]{2,1,0:T(8,128)}, ...) | async-done | bytes 116176 | tf_op jit(solution)/shard_map/psum | solution.py:449
  943.6 259.6 %all-reduce.19.cloned.1.call-done = (f32[1,112,896]{2,1,0:T(8,128)}, f32[1,112,896]{2,1,0:T(8,128)}, f32[1,112,4864]{2,1,0:T(8,128)}, f32[1,112,4864]{2,1,0:T(8,128)}, f32[1,608,896]{2,1,0:T(8,128)}) async-done(((f32[1,112,896]{2,1,0:T(8,128)}, f32[1,112,896]{2,1,0:T(8,128)}, f32[1,112,4864]{2,1,0:T(8,128)}, f32[1,112,4864]{2,1,0:T(8,128)}, f32[1,608,896]{2,1,0:T(8,128)}), (f32[1,112,896]{2,1,0:T(8,128)}, ...) | async-done | bytes 7340048 | tf_op jit(solution)/shard_map/psum | solution.py:449
  1204.5 1.8 copy.161
  1207.5 1.4 copy.163
  1210.1 1.4 copy.165
  1212.7 1.8 copy.167
  1215.6 3.1 copy.169
  1218.7 1.3 copy.170
  (232 shorter events, 46.9 us)
Async XLA Ops:
  7.2 76.7 %copy-start.2 = (bf16[1,256,896]{2,1,0:T(8,128)(2,1)S(1)}, bf16[1,256,896]{2,1,0:T(8,128)(2,1)}, u32[]{:S(2)}) copy-start(bf16[1,256,896]{2,1,0:T(8,128)(2,1)} %param.23) | copy-start | bytes 1376260
  7.2 53.1 %copy-start.28 = (s32[1,256]{1,0:T(1,128)S(1)}, s32[1,256]{1,0:T(1,128)}, u32[]{:S(2)}) copy-start(s32[1,256]{1,0:T(1,128)} %param.24) | copy-start | bytes 3076
  7.2 65.8 %copy-start.37 = (bf16[1,112,128]{2,1,0:T(8,128)(2,1)S(1)}, bf16[1,112,128]{2,1,0:T(8,128)(2,1)}, u32[]{:S(2)}) copy-start(bf16[1,112,128]{2,1,0:T(8,128)(2,1)} %param.29) | copy-start | bytes 86020
  7.2 91.7 %all-gather.19.cloned.1.call-start = ((), (), s32[]{:S(2)}) async-start(), calls=%async_computation.18 | async-start | bytes 1806336 | tf_op jit(solution)/shard_map/all_gather | solution.py:397
  7.9 124.3 %all-gather.21.cloned.1.call-start = ((), (), s32[]{:S(2)}) async-start(), calls=%async_computation.19 | async-start | bytes 1806336 | tf_op jit(solution)/shard_map/all_gather | solution.py:403
  8.7 127.3 %all-gather.27.cloned.1.call-start = ((), (), s32[]{:S(2)}) async-start(), calls=%async_computation.22 | async-start | bytes 9805824 | tf_op jit(solution)/shard_map/all_gather | solution.py:407
  9.4 171.8 %all-gather.25.cloned.1.call-start = ((), (), s32[]{:S(2)}) async-start(), calls=%async_computation.21 | async-start | bytes 9805824 | tf_op jit(solution)/shard_map/all_gather | solution.py:406
  10.0 228.7 %all-gather.23.cloned.1.call-start = ((), (), s32[]{:S(2)}) async-start(), calls=%async_computation.20 | async-start | bytes 9805824 | tf_op jit(solution)/shard_map/all_gather | solution.py:405
  10.6 328.5 %reduce-scatter.10.cloned.1.call-start = ((), (), s32[]{:S(2)}) async-start(), calls=%async_computation.9 | async-start | bytes 655360 | tf_op jit(solution)/shard_map/reduce_scatter | solution.py:319
  33.1 68.9 %copy-start.33 = (f32[896]{0:T(1024)}, f32[896]{0:T(1024)S(1)}, u32[]{:S(2)}) copy-start(f32[896]{0:T(1024)S(1)} %convert_element_type.172) | copy-start | bytes 10756
  41.7 3.2 copy-start.20
  43.6 60.0 %copy-start.35 = (f32[256]{0:T(256)}, f32[256]{0:T(256)S(1)}, u32[]{:S(2)}) copy-start(f32[256]{0:T(256)S(1)} %get-tuple-element.552) | copy-start | bytes 3076
  83.0 15.9 %copy-start.22 = (bf16[1,896,128]{2,1,0:T(8,128)(2,1)}, bf16[1,896,128]{2,1,0:T(8,128)(2,1)S(1)}, u32[]{:S(2)}) copy-start(bf16[1,896,128]{2,1,0:T(8,128)(2,1)S(1)} %all-gather.4) | copy-start | bytes 688132
  83.8 19.9 %copy-start.24 = (f32[256,32]{0,1:T(8,128)}, f32[256,32]{0,1:T(8,128)S(1)}, u32[]{:S(2)}) copy-start(f32[256,32]{0,1:T(8,128)S(1)} %get-tuple-element.550) | copy-start | bytes 98308
  130.9 5.2 copy-start.17
  132.3 2.7 copy-start.10
  134.9 0.9 copy-start.6
  136.0 102.7 %copy-start.4 = (bf16[256,896]{1,0:T(8,128)(2,1)}, bf16[256,896]{1,0:T(8,128)(2,1)S(1)}, u32[]{:S(2)}) copy-start(bf16[256,896]{1,0:T(8,128)(2,1)S(1)} %multiply_convert_fusion.3) | copy-start | bytes 1376260
  238.7 10.9 copy-start.3
  249.5 2.8 copy-start.13
  249.5 2.8 copy-start.14
  249.5 2.8 copy-start.7
  252.3 6.8 copy-start.9
  260.9 1.3 copy-start.29
  265.3 1.3 copy-start.29
  269.8 1.4 copy-start.30
  271.0 5.0 copy-start.1
  276.0 3.1 copy-start
  276.0 3.2 copy-start.26
  276.0 5.3 copy-start.31
  280.5 0.8 copy-start.27
  292.2 1.3 copy-start.30
  293.4 5.0 copy-start.1
  298.4 3.1 copy-start
  298.4 3.2 copy-start.26
  298.4 5.3 copy-start.31
  302.9 0.8 copy-start.27
  314.6 24.4 %copy-start.25 = (f32[256,32]{0,1:T(8,128)S(1)}, f32[256,32]{0,1:T(8,128)}, u32[]{:S(2)}) copy-start(f32[256,32]{0,1:T(8,128)} %copy-done.24) | copy-start | bytes 98308
  314.6 24.4 %copy-start.32 = (f32[256,32]{0,1:T(8,128)S(1)}, f32[256,32]{0,1:T(8,128)}, u32[]{:S(2)}) copy-start(f32[256,32]{0,1:T(8,128)} %get-tuple-element.548) | copy-start | bytes 98308
  314.6 25.4 %copy-start.34 = (f32[896]{0:T(1024)S(1)}, f32[896]{0:T(1024)}, u32[]{:S(2)}) copy-start(f32[896]{0:T(1024)} %copy-done.33) | copy-start | bytes 10756
  314.6 25.4 %copy-start.36 = (f32[256]{0:T(256)S(1)}, f32[256]{0:T(256)}, u32[]{:S(2)}) copy-start(f32[256]{0:T(256)} %copy-done.35) | copy-start | bytes 3076
  317.1 45.0 %reduce-scatter.12.cloned.1.call-start = ((), (), s32[]{:S(2)}) async-start(), calls=%async_computation.10 | async-start | bytes 655360 | tf_op jit(solution)/shard_map/reduce_scatter | solution.py:320
  319.1 112.7 %reduce-scatter.16.cloned.1.call-start = ((), (), s32[]{:S(2)}) async-start(), calls=%async_computation.12 | async-start | bytes 516096 | tf_op jit(solution)/shard_map/reduce_scatter | solution.py:442
  341.3 94.4 %reduce-scatter.18.cloned.1.call-start = ((), (), s32[]{:S(2)}) async-start(), calls=%async_computation.13 | async-start | bytes 516096 | tf_op jit(solution)/shard_map/reduce_scatter | solution.py:444
  364.1 3.1 copy-start.11
  364.2 121.2 %reduce-scatter.14.cloned.1.call-start = ((), (), s32[]{:S(2)}) async-start(), calls=%async_computation.11 | async-start | bytes 3612672 | tf_op jit(solution)/shard_map/reduce_scatter | solution.py:440
  367.1 2.5 copy-start.5
  367.2 168.1 %reduce-scatter.20.cloned.1.call-start = ((), (), s32[]{:S(2)}) async-start(), calls=%async_computation.14 | async-start | bytes 3612672 | tf_op jit(solution)/shard_map/reduce_scatter | solution.py:446
  369.6 288.8 %reduce-scatter.22.cloned.1.call-start = ((), (), s32[]{:S(2)}) async-start(), calls=%async_computation.15 | async-start | bytes 19611648 | tf_op jit(solution)/shard_map/reduce_scatter | solution.py:434
  379.9 401.7 %reduce-scatter.24.cloned.1.call-start = ((), (), s32[]{:S(2)}) async-start(), calls=%async_computation.16 | async-start | bytes 19611648 | tf_op jit(solution)/shard_map/reduce_scatter | solution.py:435
  390.2 1.0 copy-start.18
  390.3 514.3 %reduce-scatter.26.cloned.1.call-start = ((), (), s32[]{:S(2)}) async-start(), calls=%async_computation.17 | async-start | bytes 19611648 | tf_op jit(solution)/shard_map/reduce_scatter | solution.py:436
  401.8 1.6 copy-start.19
  401.8 1.7 copy-start.23
  401.8 2.1 copy-start.21
  401.8 541.8 %all-reduce.17.cloned.1.call-start = ((), (), s32[]{:S(2)}) async-start(), calls=%async_computation.23 | async-start | bytes 234496 | tf_op jit(solution)/shard_map/psum | solution.py:449
  407.4 497.2 %copy-start.8 = (f32[256,896]{1,0:T(8,128)S(1)}, f32[256,896]{1,0:T(8,128)}, u32[]{:S(2)}) copy-start(f32[256,896]{1,0:T(8,128)} %copy-done.6) | copy-start | bytes 2752516
  435.7 767.5 %all-reduce.19.cloned.1.call-start = ((), (), s32[]{:S(2)}) async-start(), calls=%async_computation.24 | async-start | bytes 14680064 | tf_op jit(solution)/shard_map/psum | solution.py:449
  904.6 8.0 copy-start.12
  904.6 8.0 copy-start.38
  1203.2 15.5 %copy-start.16 = (f32[1,112,4864]{2,1,0:T(8,128)S(1)}, f32[1,112,4864]{2,1,0:T(8,128)}, u32[]{:S(2)}) copy-start(f32[1,112,4864]{2,1,0:T(8,128)} %get-tuple-element.933) | copy-start | bytes 6537220
  1206.2 13.8 %copy-start.15 = (f32[1,608,896]{2,1,0:T(8,128)S(1)}, f32[1,608,896]{2,1,0:T(8,128)}, u32[]{:S(2)}) copy-start(f32[1,608,896]{2,1,0:T(8,128)} %get-tuple-element.934) | copy-start | bytes 6537220
Sparse Core Ops, SparseCore 0:
  9.9 28.7 all-gather.18
  40.6 25.6 all-gather.20
  68.2 55.6 all-gather.26
  125.6 55.6 all-gather.24
  183.0 55.6 all-gather.22
  317.2 21.8 reduce-scatter.9
  341.9 20.1 reduce-scatter.11
  365.7 32.2 reduce-scatter.15
  401.7 33.9 reduce-scatter.17
  438.9 46.4 reduce-scatter.13
  488.8 46.4 reduce-scatter.19
  538.8 119.4 reduce-scatter.21
  662.0 119.4 reduce-scatter.23
  785.0 119.4 reduce-scatter.25
  908.4 35.0 all-reduce.16
  946.2 256.9 all-reduce.18
where the time goes:
time: 1230 us
  waiting for transfers between devices  891 us (72%)
  matrix products  152 us (12%)
  blocking collectives  96.6 us (8%)
  local copies, waits for them, and re-layouts  49.5 us (4%)
  other arithmetic  19.5 us (2%)
  between operations  17.6 us (1%)
    psum x2, waiting for transfers between devices, shards(): lax.psum((layer_share[0], layer_share[1], layer_share[2], layer_share[3],...  289 us
    reduce_scatter x1, waiting for transfers between devices, shards(): lax.psum_scatter(grad_terms[10], 'fsdp', scatter_dimension=0, tiled=True)  123 us
    reduce_scatter x1, waiting for transfers between devices, shards(): lax.psum_scatter(grad_terms[11], 'fsdp', scatter_dimension=0, tiled=True)  123 us
    reduce_scatter x1, waiting for transfers between devices, shards(): lax.psum_scatter(grad_terms[9], 'fsdp', scatter_dimension=0, tiled=True)  123 us
    reduce_scatter x1, waiting for transfers between devices, shards(): lax.psum_scatter(grad_terms[7], 'fsdp', scatter_dimension=0, tiled=True)  49.9 us
    reduce_scatter x1, waiting for transfers between devices, shards(): lax.psum_scatter(grad_terms[1], 'fsdp', scatter_dimension=0, tiled=True)  49.7 us
    all_gather x1, waiting for transfers between devices, shards(): lax.all_gather(w_gate[layer_index], 'fsdp', axis=0, tiled=True)  49.5 us
    unnamed x2, blocking collectives  38.1 us
  transfers between devices with their start and end apart: 16, of which 12 were waited for; matrix products, arithmetic and copies ran while one was open for 10% of the time, Pallas kernels for 0%

commit v1 on v0

v1 whole, which is shorter than its diff:
```python
import math

import jax
import jax.numpy as jnp
from jax import lax
from jax.sharding import PartitionSpec as P

QUERY_HEADS = 14
KEY_VALUE_HEADS = 2
HEAD_SIZE = 64
ROPE_BASE = 1000000.0
EPSILON = 1e-06
NEGATIVE = -1e30
BF = jnp.bfloat16
F32 = jnp.float32


def angles(places):
    half = HEAD_SIZE // 2
    inverse = jnp.exp(jnp.arange(half, dtype=F32) * (-2.0 * math.log(ROPE_BASE) / HEAD_SIZE))
    turned = places.astype(F32)[:, None] * inverse[None, :]
    return jnp.cos(turned)[:, None, :], jnp.sin(turned)[:, None, :]


def rotate(u, cosine, sine):
    half = u.shape[-1] // 2
    a, b = u[..., :half], u[..., half:]
    return jnp.concatenate([a * cosine - b * sine, b * cosine + a * sine], axis=-1)


def norm_rows(hidden, gain):
    scale = lax.rsqrt(jnp.mean(hidden * hidden, axis=-1, keepdims=True) + EPSILON)
    return scale, (hidden * scale * gain).astype(BF)


def norm_back(hidden, scale, gain, grad):
    weighted = gain * grad
    grad_gain = jnp.sum(grad * hidden * scale, axis=0)
    inner = jnp.mean(weighted * hidden, axis=-1, keepdims=True)
    return grad_gain, scale * weighted - hidden * (scale * scale * scale) * inner


def dot(a, b):
    return jnp.dot(a, b, preferred_element_type=F32)


def dot_t(a, b):
    return lax.dot_general(a, b, (((1,), (1,)), ((), ())), preferred_element_type=F32)


def t_dot(a, b):
    return lax.dot_general(a, b, (((0,), (0,)), ((), ())), preferred_element_type=F32)


def shards(
    inputs, positions, cotangent, norm_one, w_query, b_query, key_projection, b_key,
    value_projection, value_bias, w_out, norm_two, w_gate, w_up, w_down,
):
    rows = inputs.shape[1]
    width = inputs.shape[2]
    group = QUERY_HEADS // KEY_VALUE_HEADS
    q_cols = w_query.shape[2]
    kv_cols = key_projection.shape[2]
    score_scale = 1.0 / math.sqrt(HEAD_SIZE)

    places = positions[0]
    key_places = lax.all_gather(places, "ctx", axis=0, tiled=True)
    cosine, sine = angles(places)
    hidden = inputs[0].astype(F32)

    packed = jnp.concatenate([w_query[0], key_projection[0], value_projection[0], w_out[0]], axis=1)
    packed = lax.all_gather(packed, "fsdp", axis=0, tiled=True)
    w_qkv = packed[:, : q_cols + 2 * kv_cols]
    w_o = packed[:, q_cols + 2 * kv_cols :]
    small = jnp.concatenate([norm_one[0], b_query[0], b_key[0], value_bias[0], norm_two[0]])
    small = lax.all_gather(small, "fsdp", axis=0).astype(F32)
    cuts, at = [], 0
    for piece in (norm_one, b_query, b_key, value_bias, norm_two):
        n = piece.shape[1]
        cuts.append(small[:, at : at + n].reshape(-1))
        at += n
    gain_one, bias_q, bias_k, bias_v, gain_two = cuts
    bias = jnp.concatenate([bias_q, bias_k, bias_v])

    grad_branch = cotangent[0]
    df_all = lax.all_gather(grad_branch, "fsdp", axis=0, tiled=True)
    wg = lax.all_to_all(w_gate[0], "fsdp", split_axis=1, concat_axis=0, tiled=True)
    wu = lax.all_to_all(w_up[0], "fsdp", split_axis=1, concat_axis=0, tiled=True)
    wd = w_down[0]

    scale_one, normed = norm_rows(hidden, gain_one)
    qkv = dot(normed, w_qkv) + bias
    q = rotate(qkv[:, :q_cols].reshape(rows, QUERY_HEADS, HEAD_SIZE), cosine, sine).astype(BF)
    k = rotate(
        qkv[:, q_cols : q_cols + kv_cols].reshape(rows, KEY_VALUE_HEADS, HEAD_SIZE), cosine, sine
    ).astype(BF)
    v = qkv[:, q_cols + kv_cols :].astype(BF)
    kv = jnp.concatenate([k.reshape(rows, kv_cols), v], axis=1)
    kv = lax.all_gather(kv, "ctx", axis=0, tiled=True)
    total = kv.shape[0]
    k_all = kv[:, :kv_cols].reshape(total, KEY_VALUE_HEADS, HEAD_SIZE)
    v_all = kv[:, kv_cols:].reshape(total, KEY_VALUE_HEADS, HEAD_SIZE)
    q = q.reshape(rows, KEY_VALUE_HEADS, group, HEAD_SIZE)
    s = jnp.einsum("tgjd,ugd->gjtu", q, k_all, preferred_element_type=F32) * score_scale
    s = jnp.where(key_places[None, :] <= places[:, None], s, NEGATIVE)
    top = jnp.max(s, axis=-1, keepdims=True)
    lse = top + jnp.log(jnp.sum(jnp.exp(s - top), axis=-1, keepdims=True))
    pf = jnp.exp(s - lse)
    p = pf.astype(BF)
    o = jnp.einsum("gjtu,ugd->tgjd", p, v_all, preferred_element_type=F32)
    ob = o.reshape(rows, q_cols).astype(BF)
    middle = hidden + dot(ob, w_o)
    scale_two, normed_two = norm_rows(middle, gain_two)

    x_all = lax.all_gather(normed_two, "fsdp", axis=0, tiled=True)
    gate = dot(x_all, wg)
    up = dot(x_all, wu)
    sig = jax.nn.sigmoid(gate)
    hid = (gate * sig * up).astype(BF)
    out_part = dot(hid, wd).astype(BF)
    ffn_out = lax.psum_scatter(out_part, "fsdp", scatter_dimension=0, tiled=True)
    output = middle + ffn_out.astype(F32)

    dhid = dot_t(df_all, wd)
    dgate = (dhid * up * sig * (1.0 + gate * (1.0 - sig))).astype(BF)
    dup = (dhid * (gate * sig)).astype(BF)
    dx_part = (dot_t(dgate, wg) + dot_t(dup, wu)).astype(BF)
    dxn2 = lax.psum_scatter(dx_part, "fsdp", scatter_dimension=0, tiled=True).astype(F32)
    g_down = t_dot(hid, df_all)
    g_gate = t_dot(x_all, dgate)
    g_up = t_dot(x_all, dup)

    g_out = grad_branch.astype(F32)
    grad_gain_two, dmid = norm_back(middle, scale_two, gain_two, dxn2)
    dm = g_out + dmid
    da = dm.astype(BF)
    g_wo = t_dot(ob, da)
    dob = dot_t(da, w_o).astype(BF).reshape(rows, KEY_VALUE_HEADS, group, HEAD_SIZE)

    dp = jnp.einsum("tgjd,ugd->gjtu", dob, v_all, preferred_element_type=F32)
    delta = jnp.sum(pf * dp, axis=-1, keepdims=True)
    ds = (pf * (dp - delta)).astype(BF)
    dq = jnp.einsum("gjtu,ugd->tgjd", ds, k_all, preferred_element_type=F32) * score_scale
    dk = jnp.einsum("gjtu,tgjd->ugd", ds, q, preferred_element_type=F32) * score_scale
    dv = jnp.einsum("gjtu,tgjd->ugd", p, dob, preferred_element_type=F32)
    dkv = jnp.concatenate([dk.reshape(total, kv_cols), dv.reshape(total, kv_cols)], axis=1)
    dkv = lax.psum_scatter(dkv, "ctx", scatter_dimension=0, tiled=True)
    dq = rotate(dq.reshape(rows, QUERY_HEADS, HEAD_SIZE), cosine, -sine).astype(BF)
    dk = rotate(
        dkv[:, :kv_cols].reshape(rows, KEY_VALUE_HEADS, HEAD_SIZE), cosine, -sine
    ).astype(BF)
    dqkv = jnp.concatenate(
        [dq.reshape(rows, q_cols), dk.reshape(rows, kv_cols), dkv[:, kv_cols:].astype(BF)], axis=1
    )
    g_qkv = t_dot(normed, dqkv)
    g_bias = jnp.sum(dqkv.astype(F32), axis=0)
    dxn = dot_t(dqkv, w_qkv)
    grad_gain_one, dhidden = norm_back(hidden, scale_one, gain_one, dxn)
    grad_in = dm + dhidden

    g_attn = jnp.concatenate([g_qkv, g_wo], axis=1).astype(BF)
    g_attn = lax.psum_scatter(g_attn, "fsdp", scatter_dimension=0, tiled=True)
    back = [
        lax.all_to_all(g.astype(BF), "fsdp", split_axis=0, concat_axis=1, tiled=True)
        for g in (g_gate, g_up)
    ]
    g_attn, g_gate, g_up, g_down = lax.psum((g_attn, back[0], back[1], g_down.astype(BF)), "ctx")
    pieces = jnp.concatenate(
        [
            g.reshape(small.shape[0], -1)
            for g in (
                grad_gain_one, g_bias[:q_cols], g_bias[q_cols : q_cols + kv_cols],
                g_bias[q_cols + kv_cols :], grad_gain_two,
            )
        ],
        axis=1,
    )
    pieces = lax.psum(pieces, ("ctx", "fsdp"))
    mine = lax.dynamic_slice_in_dim(pieces, lax.axis_index("fsdp"), 1, axis=0)
    outs, at = [], 0
    for piece in (norm_one, b_query, b_key, value_bias, norm_two):
        n = piece.shape[1]
        outs.append(mine[:, at : at + n])
        at += n
    g_n1, g_bq, g_bk, g_bv, g_n2 = outs
    g_attn = g_attn.astype(F32)
    return (
        output[None], grad_in[None], g_n1,
        g_attn[None, :, :q_cols], g_bq,
        g_attn[None, :, q_cols : q_cols + kv_cols], g_bk,
        g_attn[None, :, q_cols + kv_cols : q_cols + 2 * kv_cols], g_bv,
        g_attn[None, :, q_cols + 2 * kv_cols :], g_n2,
        g_gate.astype(F32)[None], g_up.astype(F32)[None], g_down.astype(F32)[None],
    )


def solution(mesh):
    tok, row, vec = P("fsdp", "ctx", None), P(None, "fsdp", None), P(None, "fsdp")
    return jax.shard_map(
        shards,
        mesh=mesh,
        in_specs=(
            tok, P("fsdp", "ctx"), tok, vec, row, vec, row, vec, row, vec, row, vec, row, row, row,
        ),
        out_specs=(tok, tok, vec, row, vec, row, vec, row, vec, row, vec, row, row, row),
        check_vma=False,
    )
```

time: 1230 us -> 597 us (0.49)
  waiting for transfers between devices: 891 us -> 294 us
  matrix products: 152 us -> 109 us
  local copies, waits for them, and re-layouts: 49.5 us -> 29.9 us
  other arithmetic: 19.5 us -> 36.6 us
  starting transfers between devices: 0.86 us -> 16.4 us
    reduce_scatter x9 -> x4, waiting for transfers between devices: 513 us -> 114 us  [the longest x1 50.6 us: shards(): lax.psum_scatter(out_part, 'fsdp', scatter_dimension=0, tiled=True)]
    psum x2 -> x1, waiting for transfers between devices: 289 us -> 91.5 us  [shards(): lax.psum((g_attn, back[0], back[1], g_down.astype(BF)), 'ctx')]
    dot_general x39 -> x21, matrix products: 152 us -> 109 us  [the longest x5 26.4 us: dot(): return jnp.dot(a, b, preferred_element_type=F32)]
    psum x0 -> x1, blocking collectives: none -> 42.5 us  [shards(): pieces = lax.psum(pieces, ('ctx', 'fsdp'))]
    all_to_all x0 -> x4, waiting for transfers between devices: none -> 39.1 us  [the longest x2 23.9 us: shards(): lax.all_to_all(g.astype(BF), 'fsdp', split_axis=0, concat_axis=1, tiled=T...]
    all_gather x5 -> x3, waiting for transfers between devices: 84.8 us -> 48.9 us  [the longest x1 25 us: shards(): df_all = lax.all_gather(grad_branch, 'fsdp', axis=0, tiled=True)]
    all_gather x4 -> x1, blocking collectives: 46.9 us -> 16 us  [shards(): kv = lax.all_gather(kv, 'ctx', axis=0, tiled=True)]
    unnamed x91 -> x57, local copies, waits for them, and re-layouts: 29.5 us -> 2.19 us
  transfers between devices with their start and end apart: 16 -> 12, of which waited for: 12 -> 10; matrix products, arithmetic and copies ran while one was open for 10% -> 12% of each run, Pallas kernels for 0% -> 0%
where the time goes in v1:
time: 597 us; the launch traced here: 588 us
  waiting for transfers between devices  294 us (49%)
  matrix products  109 us (18%)
  blocking collectives  85.6 us (14%)
  other arithmetic  36.6 us (6%)
  local copies, waits for them, and re-layouts  29.9 us (5%)
  starting transfers between devices  16.4 us (3%)
  between operations  15.9 us (3%)
    psum x1, waiting for transfers between devices, shards(): lax.psum((g_attn, back[0], back[1], g_down.astype(BF)), 'ctx')  91.5 us
    reduce_scatter x1, waiting for transfers between devices, shards(): lax.psum_scatter(out_part, 'fsdp', scatter_dimension=0, tiled=True)  50.6 us
    psum x1, blocking collectives, shards(): pieces = lax.psum(pieces, ('ctx', 'fsdp'))  42.5 us
    reduce_scatter x1, waiting for transfers between devices, shards(): lax.psum_scatter(dx_part, 'fsdp', scatter_dimension=0, tiled=True)  41.4 us
    dot_general x5, matrix products, dot(): return jnp.dot(a, b, preferred_element_type=F32)  26.4 us
    all_gather x1, waiting for transfers between devices, shards(): df_all = lax.all_gather(grad_branch, 'fsdp', axis=0, tiled=True)  25 us
    all_to_all x2, waiting for transfers between devices, shards(): lax.all_to_all(g.astype(BF), 'fsdp', split_axis=0, concat_axis=1, tiled=T...  23.9 us
    dot_general x5, matrix products, dot_t(): lax.dot_general(a, b, (((1,), (1,)), ((), ())), preferred_element_type=F32)  23.6 us
  transfers between devices with their start and end apart: 12, of which 10 were waited for; matrix products, arithmetic and copies ran while one was open for 12% of the time, Pallas kernels for 0%

profile of v1, /device:TPU:0, one launch (start us, length us, event | category | flops | bytes accessed | tf_op | source)
XLA Modules:
  0.0 587.7 jit_solution(11810509420019293082)
XLA Ops:
  7.2 2.0 pad_maximum_fusion.3
  10.0 1.2 dynamic-slice
  11.9 3.4 concatenate.46
  15.5 15.6 %all-reduce = bf16[2944]{0:T(1024)(128)(2,1)S(1)} all-reduce(bf16[2944]{0:T(1024)(128)(2,1)S(1)} %dynamic-update-slice), channel_id=2, replica_groups=mesh['ctx'=4,'fsdp'=8] {'fsdp'}, use_global_device_ids=true, to_apply=%add | all-reduce | flops 2944 | bytes 11776
  31.8 11.4 %all-gather.1 = s32[1,1024]{1,0:T(1,128)S(1)} all-gather(s32[1,256]{1,0:T(1,128)} %param.16), channel_id=3, replica_groups=mesh['ctx'=4,'fsdp'=8] {'ctx'}, dimensions={1}, use_global_device_ids=true | all-gather | bytes 5120 | tf_op jit(solution)/shard_map/all_gather | solution.py:67
  43.2 1.2 fusion.38
  45.6 2.3 all-gather.7.cloned.1.call-done
  47.8 2.6 convolution_add_fusion
  51.3 16.0 %all_gather.24 = bf16[1024,256]{1,0:T(8,128)(2,1)S(1)} all-gather(bf16[256,256]{1,0:T(8,128)(2,1)S(1)} %pad_maximum_fusion.8), channel_id=1, replica_groups=mesh['ctx'=4,'fsdp'=8] {'ctx'}, dimensions={0}, use_global_device_ids=true | all-gather | bytes 655360 | tf_op jit(solution)/shard_map/all_gather | solution.py:99
  67.8 6.5 %fusion.4 = (f32[2,7,256]{2,1,0:T(8,128)S(1)}, f32[2,1024,256,7]{2,1,3,0:T(8,128)}) fusion(pred[256,1024]{0,1:T(8,128)(4,1)S(1)} %broadcast_compare_fusion, bf16[1024,2,64,1]{0,2,3,1:T(8,128)(2,1)S(1)} %bitcast.159, bf16[256,2,7,32]{0,3,2,1:T(8,128)(2,1)S(1)} %bitcast.164, bf16[256,2,7,32]{0,3,2,1:T(8,128)(2,1)S(1)} %bitcast.162), kind=kOutput, calls=%fused_computation.9 | convolution fusion | flops 481686016 | bytes 15677440 | tf_op jit(solution)/shard_map/tgjd,ugd->gjtu/dot_general | solution.py:104
  74.2 8.2 %exponential_reduce_fusion = f32[2,7,256]{2,1,0:T(8,128)S(1)} fusion(f32[2,1024,256,7]{2,1,3,0:T(8,128)} %get-tuple-element.61, f32[2,7,256]{2,1,0:T(8,128)S(1)} %get-tuple-element.60, pred[256,1024]{0,1:T(8,128)(4,1)S(1)} %broadcast_compare_fusion), kind=kLoop, calls=%fused_computation.7 | loop fusion | flops 14676480 | bytes 14970880 | tf_op jit(solution)/shard_map/reduce_sum | solution.py:107
  82.5 7.1 %convolution_convert_fusion.5 = bf16[2,64,7,256]{3,1,2,0:T(8,128)(2,1)S(1)} fusion(bf16[1024,2,64,1]{0,2,3,1:T(8,128)(2,1)S(1)} %bitcast.173, f32[2,1024,256,7]{2,1,3,0:T(8,128)} %get-tuple-element.61, f32[2,7,256]{2,1,0:T(8,128)S(1)} %log_add_fusion, pred[256,1024]{0,1:T(8,128)(4,1)S(1)} %broadcast_compare_fusion), kind=kOutput, calls=%fused_computation.44 | convolution fusion | flops 484671488 | bytes 15677440 | tf_op jit(solution)/shard_map/gjtu,ugd->tgjd/dot_general | solution.py:110
  89.6 2.4 multiply_reduce_fusion
  92.0 0.9 multiply_convert_fusion.3
  93.7 3.1 all_to_all.60
  96.8 1.1 copy.70
  97.9 4.7 all-to-all-start.1
  102.7 3.1 all_to_all.56
  105.8 1.1 copy.69
  106.9 15.1 %all-to-all-done.1 = bf16[112,8,608]{2,0,1:T(8,128)(2,1)} async-done(((bf16[112,8,608]{2,0,1:T(8,128)(2,1)}), bf16[112,8,608]{2,0,1:T(8,128)(2,1)}, u32[]{:S(2)}, u32[]{:S(2)}) %all-to-all-start.1) | async-done | bytes 1089568 | tf_op jit(solution)/shard_map/all_to_all | solution.py:88
  122.0 3.6 all-to-all-start
  125.7 21.7 %all-gather.9.cloned.1.call-done = bf16[2048,896]{1,0:T(8,128)(2,1)} async-done(((bf16[256,896]{1,0:T(8,128)(2,1)}), bf16[2048,896]{1,0:T(8,128)(2,1)}) %all-gather.9.cloned.1.call-update) | async-done | bytes 3670032 | tf_op jit(solution)/shard_map/all_gather | solution.py:115
  147.4 7.4 %fusion.70 = f32[2048,608]{0,1:T(8,128)} fusion(bf16[2048,896]{1,0:T(8,128)(2,1)} %all-gather.9.cloned.1.call-done, bf16[896,608]{1,0:T(8,128)(2,1)} %bitcast.31), kind=kOutput, calls=%fused_computation.125 | convolution fusion | flops 2231369728 | bytes 9740288 | tf_op jit(solution)/shard_map/dot_general | solution.py:44
  154.7 7.1 %fusion.69 = f32[2048,608]{0,1:T(8,128)} fusion(bf16[2048,896]{1,0:T(8,128)(2,1)} %all-gather.9.cloned.1.call-done, bf16[896,608]{1,0:T(8,128)(2,1)S(1)} %bitcast.171), kind=kOutput, calls=%fused_computation.124 | convolution fusion | flops 2231369728 | bytes 9740288 | tf_op jit(solution)/shard_map/dot_general | solution.py:44
  161.8 25.0 %all-gather.11.cloned.1.call-done = bf16[1,2048,896]{2,1,0:T(8,128)(2,1)} async-done(((bf16[1,256,896]{2,1,0:T(8,128)(2,1)}), bf16[1,2048,896]{2,1,0:T(8,128)(2,1)}) %all-gather.11.cloned.1.call-update) | async-done | bytes 3670032 | tf_op jit(solution)/shard_map/all_gather | solution.py:86
  186.8 9.2 %multiply_convert_fusion = (bf16[2048,608]{0,1:T(8,128)(2,1)S(1)}, bf16[2048,608]{0,1:T(8,128)(2,1)S(1)}, bf16[2048,608]{0,1:T(8,128)(2,1)}) fusion(f32[2048,608]{0,1:T(8,128)} %fusion.69, f32[2048,608]{0,1:T(8,128)} %fusion.70, bf16[1,608,896]{2,1,0:T(8,128)(2,1)S(1)} %copy-done, bf16[1,2048,896]{2,1,0:T(8,128)(2,1)} %all-gather.11.cloned.1.call-done), kind=kOutput, calls=%fused_computation.11 | convolution fusion | flops 2250047488 | bytes 22192128 | tf_op jit(solution)/shard_map/dot_general | solution.py:48
  196.0 3.4 fusion.71
  199.4 6.2 %add_convert_fusion = bf16[2048,896]{1,0:T(8,128)(2,1)} fusion(f32[2048,896]{1,0:T(8,128)S(1)} %fusion.71, bf16[2048,608]{0,1:T(8,128)(2,1)S(1)} %get-tuple-element.22, bf16[896,608]{1,0:T(8,128)(2,1)} %bitcast.31), kind=kOutput, calls=%fused_computation.10 | convolution fusion | flops 2235039744 | bytes 14589952 | tf_op jit(solution)/shard_map/dot_general | solution.py:48
  205.6 6.9 %convolution_convert_fusion = bf16[2048,896]{1,0:T(8,128)(2,1)} fusion(bf16[2048,608]{0,1:T(8,128)(2,1)} %get-tuple-element.24, bf16[1,608,896]{2,1,0:T(8,128)(2,1)S(1)} %copy-done), kind=kOutput, calls=%fused_computation.21 | convolution fusion | flops 2233204736 | bytes 7249920 | tf_op jit(solution)/shard_map/dot_general | solution.py:44
  212.9 41.4 %reduce-scatter.7.cloned.1.call-done = bf16[256,896]{1,0:T(8,128)(2,1)} async-done(((bf16[2048,896]{1,0:T(8,128)(2,1)}), bf16[256,896]{1,0:T(8,128)(2,1)}) %reduce-scatter.7.cloned.1.call-update) | async-done | bytes 458768 | tf_op jit(solution)/shard_map/reduce_scatter | solution.py:128
  254.3 1.3 fusion.37
  255.6 50.6 %reduce-scatter.5.cloned.1.call-done = bf16[256,896]{1,0:T(8,128)(2,1)} async-done(((bf16[2048,896]{1,0:T(8,128)(2,1)}), bf16[256,896]{1,0:T(8,128)(2,1)}) %reduce-scatter.5.cloned.1.call-update) | async-done | bytes 458768 | tf_op jit(solution)/shard_map/reduce_scatter | solution.py:121
  306.2 2.4 fusion.34
  308.6 2.2 fusion.25
  311.0 7.2 %fusion.53 = f32[2,64,1024,1]{2,1,3,0:T(8,128)S(1)} fusion(bf16[256,2,7,64]{0,3,2,1:T(8,128)(2,1)S(1)} %bitcast.166, f32[2,1024,256,7]{2,1,3,0:T(8,128)} %get-tuple-element.61, f32[2,7,256]{2,1,0:T(8,128)S(1)} %log_add_fusion, pred[256,1024]{0,1:T(8,128)(4,1)S(1)} %broadcast_compare_fusion), kind=kOutput, calls=%fused_computation.98 | convolution fusion | flops 484442112 | bytes 15939584 | tf_op jit(solution)/shard_map/gjtu,tgjd->ugd/dot_general | solution.py:145
  318.2 11.5 %fusion = (f32[2,7,256]{2,1,0:T(8,128)S(1)}, f32[2,1024,256,7]{2,1,3,0:T(8,128)}) fusion(f32[2,1024,256,7]{2,1,3,0:T(8,128)} %get-tuple-element.61, f32[2,7,256]{2,1,0:T(8,128)S(1)} %log_add_fusion, pred[256,1024]{0,1:T(8,128)(4,1)S(1)} %broadcast_compare_fusion, bf16[1024,2,64,1]{0,2,3,1:T(8,128)(2,1)S(1)} %bitcast.174, ...), kind=kOutput, calls=%fused_computation.2 | convolution fusion | flops 488108544 | bytes 30371840 | tf_op jit(solution)/shard_map/tgjd,ugd->gjtu/dot_general | solution.py:140
  329.8 7.8 %fusion.2 = bf16[2,7,256,1024]{2,3,1,0:T(8,128)(2,1)S(1)} fusion(f32[2,1024,256,7]{2,1,3,0:T(8,128)} %get-tuple-element.65, f32[2,1024,256,7]{2,1,3,0:T(8,128)S(1)} %bitcast.154, f32[2,7,256]{2,1,0:T(8,128)S(1)} %get-tuple-element.64, f32[2,7,256]{2,1,0:T(8,128)S(1)} %log_add_fusion, pred[256,1024]{0,1:T(8,128)(4,1)S(1)} %broadcast_compare_fusion), kind=kLoop, calls=%fused_computation.4 | loop fusion | flops 22020096 | bytes 36990976 | tf_op jit(solution)/shard_map/convert_element_type | solution.py:142
  337.7 2.3 fusion.28
  340.6 1.0 pad_maximum_fusion.1
  342.0 4.5 convolution_multiply_fusion
  347.3 21.7 %reduce-scatter.9.cloned.1.call-done = f32[256,256]{0,1:T(8,128)} async-done(((f32[1024,256]{0,1:T(8,128)}), f32[256,256]{0,1:T(8,128)}) %reduce-scatter.9.cloned.1.call-update) | async-done | bytes 262160 | tf_op jit(solution)/shard_map/reduce_scatter | solution.py:147
  371.0 1.9 convolution_convert_fusion.1
  372.9 2.3 pad_maximum_fusion
  375.2 5.5 convolution_convert_fusion.4
  380.8 1.4 copy.76
  382.2 3.6 all-to-all-start.2
  385.9 5.7 convolution_convert_fusion.3
  391.6 1.4 copy.78
  393.0 13.5 %all-to-all-done.2 = bf16[8,112,608]{2,1,0:T(8,128)(2,1)S(1)} async-done(((bf16[8,112,608]{2,1,0:T(8,128)(2,1)}), bf16[8,112,608]{2,1,0:T(8,128)(2,1)S(1)}, u32[]{:S(2)}, u32[]{:S(2)}) %all-to-all-start.2) | async-done | bytes 1089568 | tf_op jit(solution)/shard_map/all_to_all | solution.py:164
  406.5 3.6 all-to-all-start.3
  410.1 6.6 %fusion.20 = bf16[1,608,896]{2,1,0:T(8,128)(2,1)} fusion(bf16[2048,608]{0,1:T(8,128)(2,1)} %get-tuple-element.24, bf16[1,2048,896]{2,1,0:T(8,128)(2,1)} %all-gather.11.cloned.1.call-done), kind=kOutput, calls=%fused_computation.41 | convolution fusion | flops 2231914496 | bytes 7249920 | tf_op jit(solution)/shard_map/dot_general | solution.py:52
  416.6 1.2 copy.77
  417.9 3.0 broadcast_in_dim.65
  420.8 10.5 %all-to-all-done.3 = bf16[8,112,608]{2,1,0:T(8,128)(2,1)S(1)} async-done(((bf16[8,112,608]{2,1,0:T(8,128)(2,1)}), bf16[8,112,608]{2,1,0:T(8,128)(2,1)S(1)}, u32[]{:S(2)}, u32[]{:S(2)}) %all-to-all-start.3) | async-done | bytes 1089568 | tf_op jit(solution)/shard_map/all_to_all | solution.py:164
  431.6 1.7 broadcast_in_dim.67
  433.4 2.7 fusion.47
  436.8 42.5 %psum.35 = f32[8,368]{1,0:T(8,128)S(1)} all-reduce(f32[8,368]{1,0:T(8,128)S(1)} %concatenate.58), channel_id=1, replica_groups=mesh['ctx'=4,'fsdp'=8] {'ctx','fsdp'}, use_global_device_ids=true, to_apply=%region_13.14 | all-reduce | flops 2944 | bytes 23552 | tf_op jit(solution)/shard_map/psum | solution.py:178
  480.4 1.2 fusion.44
  481.6 91.5 %all-reduce.4.cloned.1.call-done = (bf16[112,2048]{1,0:T(8,128)(2,1)}, bf16[1,112,4864]{2,1,0:T(8,128)(2,1)}, bf16[1,112,4864]{2,1,0:T(8,128)(2,1)}, bf16[1,608,896]{2,1,0:T(8,128)(2,1)}) async-done(((bf16[112,2048]{1,0:T(8,128)(2,1)}, bf16[1,112,4864]{2,1,0:T(8,128)(2,1)}, bf16[1,112,4864]{2,1,0:T(8,128)(2,1)}, bf16[1,608,896]{2,1,0:T(8,128)(2,1)}), (bf16[112,2048]{1,0:T(8,128)(2,1)}, ...) | async-done | bytes 3727376 | tf_op jit(solution)/shard_map/psum | solution.py:167
  573.1 1.2 convert_element_type.130
  575.0 0.9 slice_bitcast_fusion
  575.9 1.5 broadcast_in_dim.66
  577.4 1.5 broadcast_in_dim.68
  578.9 1.5 broadcast_in_dim.70
  (127 shorter events, 11.7 us)
Async XLA Ops:
  7.2 179.6 %copy-start = (bf16[1,608,896]{2,1,0:T(8,128)(2,1)S(1)}, bf16[1,608,896]{2,1,0:T(8,128)(2,1)}, u32[]{:S(2)}) copy-start(bf16[1,608,896]{2,1,0:T(8,128)(2,1)} %param.29) | copy-start | bytes 3268612
  7.2 40.6 %all-gather.7.cloned.1.call-start = ((), (), s32[]{:S(2)}) async-start(), calls=%async_computation.8 | async-start | bytes 4128768 | tf_op jit(solution)/shard_map/all_gather | solution.py:72
  9.2 138.2 %all-gather.9.cloned.1.call-start = ((), (), s32[]{:S(2)}) async-start(), calls=%async_computation.9 | async-start | bytes 4128768 | tf_op jit(solution)/shard_map/all_gather | solution.py:115
  51.1 23.1 %copy-start.5 = (bf16[256,14,32]{0,2,1:T(8,128)(2,1)}, bf16[256,14,32]{0,2,1:T(8,128)(2,1)S(1)}, u32[]{:S(2)}) copy-start(bf16[256,14,32]{0,2,1:T(8,128)(2,1)S(1)} %get-tuple-element.27) | copy-start | bytes 688132
  51.1 23.1 %copy-start.7 = (bf16[256,14,32]{0,2,1:T(8,128)(2,1)}, bf16[256,14,32]{0,2,1:T(8,128)(2,1)S(1)}, u32[]{:S(2)}) copy-start(bf16[256,14,32]{0,2,1:T(8,128)(2,1)S(1)} %get-tuple-element.28) | copy-start | bytes 688132
  67.6 6.7 %copy-start.3 = (bf16[1024,128]{0,1:T(8,128)(2,1)}, bf16[1024,128]{0,1:T(8,128)(2,1)S(1)}, u32[]{:S(2)}) copy-start(bf16[1024,128]{0,1:T(8,128)(2,1)S(1)} %copy.66) | copy-start | bytes 786436
  67.7 14.7 %copy-start.17 = (bf16[1024,128]{0,1:T(8,128)(2,1)}, bf16[1024,128]{0,1:T(8,128)(2,1)S(1)}, u32[]{:S(2)}) copy-start(bf16[1024,128]{0,1:T(8,128)(2,1)S(1)} %copy.65) | copy-start | bytes 786436
  82.5 7.1 %copy-start.12 = (bf16[1,256,896]{2,1,0:T(8,128)(2,1)S(1)}, bf16[1,256,896]{2,1,0:T(8,128)(2,1)}, u32[]{:S(2)}) copy-start(bf16[1,256,896]{2,1,0:T(8,128)(2,1)} %param.15) | copy-start | bytes 1376260
  89.6 3.5 copy-start.19
  93.0 93.8 %all-gather.11.cloned.1.call-start = ((), (), s32[]{:S(2)}) async-start(), calls=%async_computation.14 | async-start | bytes 4128768 | tf_op jit(solution)/shard_map/all_gather | solution.py:86
  97.9 24.1 %all-to-all-start.1 = ((bf16[112,8,608]{2,0,1:T(8,128)(2,1)}), bf16[112,8,608]{2,0,1:T(8,128)(2,1)}, u32[]{:S(2)}, u32[]{:S(2)}) async-start(bf16[112,8,608]{2,0,1:T(8,128)(2,1)} %copy.70), calls=%async_computation.1 | async-start | bytes 2293760 | tf_op jit(solution)/shard_map/all_to_all | solution.py:88
  122.0 32.7 %all-to-all-start = ((bf16[112,8,608]{2,0,1:T(8,128)(2,1)}), bf16[112,8,608]{2,0,1:T(8,128)(2,1)S(1)}, u32[]{:S(2)}, u32[]{:S(2)}) async-start(bf16[112,8,608]{2,0,1:T(8,128)(2,1)} %copy.69), calls=%async_computation | async-start | bytes 2293760 | tf_op jit(solution)/shard_map/all_to_all | solution.py:87
  125.7 128.6 %reduce-scatter.7.cloned.1.call-start = ((), (), s32[]{:S(2)}) async-start(), calls=%async_computation.11 | async-start | bytes 4128768 | tf_op jit(solution)/shard_map/reduce_scatter | solution.py:128
  196.0 3.4 copy-start.21
  196.0 3.4 copy-start.22
  205.6 100.6 %reduce-scatter.5.cloned.1.call-start = ((), (), s32[]{:S(2)}) async-start(), calls=%async_computation.10 | async-start | bytes 4128768 | tf_op jit(solution)/shard_map/reduce_scatter | solution.py:121
  212.6 93.6 %copy-start.9 = (bf16[1,256,896]{2,1,0:T(8,128)(2,1)S(1)}, bf16[1,256,896]{2,1,0:T(8,128)(2,1)}, u32[]{:S(2)}) copy-start(bf16[1,256,896]{2,1,0:T(8,128)(2,1)} %param.17) | copy-start | bytes 1376260
  212.6 156.5 %reduce-scatter.9.cloned.1.call-start = ((), (), s32[]{:S(2)}) async-start(), calls=%async_computation.12 | async-start | bytes 1310720 | tf_op jit(solution)/shard_map/reduce_scatter | solution.py:147
  311.0 7.2 %copy-start.18 = (bf16[1024,128]{0,1:T(8,128)(2,1)S(1)}, bf16[1024,128]{0,1:T(8,128)(2,1)}, u32[]{:S(2)}) copy-start(bf16[1024,128]{0,1:T(8,128)(2,1)} %copy-done.17) | copy-start | bytes 786436
  311.0 18.8 %slice-start = ((s8[14680064]{0:T(1024)(128)(4,1)}), s8[4194304]{0:T(1024)(128)(4,1)S(1)}, s32[]{:S(2)}) async-start(s8[14680064]{0:T(1024)(128)(4,1)} %bitcast.153), calls=%async_computation.16 | async-start | bytes 8388608
  311.0 18.7 %slice-start.1 = ((s8[14680064]{0:T(1024)(128)(4,1)}), s8[2097152]{0:T(1024)(128)(4,1)S(1)}, s32[]{:S(2)}) async-start(s8[14680064]{0:T(1024)(128)(4,1)} %bitcast.153), calls=%async_computation.17 | async-start | bytes 4194304
  318.2 11.5 %slice-start.2 = ((s8[14680064]{0:T(1024)(128)(4,1)}), s8[4194304]{0:T(1024)(128)(4,1)S(1)}, s32[]{:S(2)}) async-start(s8[14680064]{0:T(1024)(128)(4,1)} %bitcast.153), calls=%async_computation.18 | async-start | bytes 8388608
  318.2 11.5 %slice-start.3 = ((s8[14680064]{0:T(1024)(128)(4,1)}), s8[4194304]{0:T(1024)(128)(4,1)S(1)}, s32[]{:S(2)}) async-start(s8[14680064]{0:T(1024)(128)(4,1)} %bitcast.153), calls=%async_computation.19 | async-start | bytes 8388608
  329.8 7.8 %copy-start.6 = (bf16[256,14,32]{0,2,1:T(8,128)(2,1)S(1)}, bf16[256,14,32]{0,2,1:T(8,128)(2,1)}, u32[]{:S(2)}) copy-start(bf16[256,14,32]{0,2,1:T(8,128)(2,1)} %copy-done.5) | copy-start | bytes 688132
  329.8 7.8 %copy-start.8 = (bf16[256,14,32]{0,2,1:T(8,128)(2,1)S(1)}, bf16[256,14,32]{0,2,1:T(8,128)(2,1)}, u32[]{:S(2)}) copy-start(bf16[256,14,32]{0,2,1:T(8,128)(2,1)} %copy-done.7) | copy-start | bytes 688132
  337.7 2.9 copy-start.2
  337.7 4.3 copy-start.4
  341.6 91.7 %reduce-scatter.11.cloned.1.call-start = ((), (), s32[]{:S(2)}) async-start(), calls=%async_computation.13 | async-start | bytes 4128768 | tf_op jit(solution)/shard_map/reduce_scatter | solution.py:162
  341.9 4.7 copy-start.20
  346.7 26.2 %copy-start.10 = (bf16[256,14,64]{0,2,1:T(8,128)(2,1)}, bf16[256,14,64]{0,2,1:T(8,128)(2,1)S(1)}, u32[]{:S(2)}) copy-start(bf16[256,14,64]{0,2,1:T(8,128)(2,1)S(1)} %pad_maximum_fusion.5) | copy-start | bytes 1376260
  382.2 24.3 %all-to-all-start.2 = ((bf16[8,112,608]{2,1,0:T(8,128)(2,1)}), bf16[8,112,608]{2,1,0:T(8,128)(2,1)S(1)}, u32[]{:S(2)}, u32[]{:S(2)}) async-start(bf16[8,112,608]{2,1,0:T(8,128)(2,1)} %bitcast.64), calls=%async_computation.6 | async-start | bytes 2293760 | tf_op jit(solution)/shard_map/all_to_all | solution.py:164
  406.5 24.9 %all-to-all-start.3 = ((bf16[8,112,608]{2,1,0:T(8,128)(2,1)}), bf16[8,112,608]{2,1,0:T(8,128)(2,1)S(1)}, u32[]{:S(2)}, u32[]{:S(2)}) async-start(bf16[8,112,608]{2,1,0:T(8,128)(2,1)} %bitcast.66), calls=%async_computation.7 | async-start | bytes 2293760 | tf_op jit(solution)/shard_map/all_to_all | solution.py:164
  410.0 163.1 %all-reduce.4.cloned.1.call-start = ((), (), s32[]{:S(2)}) async-start(), calls=%async_computation.15 | async-start | bytes 7454720 | tf_op jit(solution)/shard_map/psum | solution.py:167
  431.5 1.9 copy-start.11
  431.6 1.9 copy-start.13
  573.1 2.9 copy-start.16
  573.1 4.3 copy-start.15
  575.9 3.0 copy-start.14
  575.9 4.5 copy-start.1
Sparse Core Ops, SparseCore 0:
  10.5 37.3 all-gather.6
  93.1 54.2 all-gather.8
  149.3 37.4 all-gather.10
  205.7 48.5 reduce-scatter.6
  257.6 48.5 reduce-scatter.4
  341.8 27.2 reduce-scatter.8
  375.4 56.0 reduce-scatter.10
  434.7 138.3 all-reduce.3

commit v2 on v1

--- a/solution.py
+++ b/solution.py
@@ -1,8 +1,11 @@
+import functools
 import math
 
 import jax
 import jax.numpy as jnp
 from jax import lax
+from jax.experimental import pallas as pl
+from jax.experimental.pallas import tpu as pltpu
 from jax.sharding import PartitionSpec as P
 
 QUERY_HEADS = 14
@@ -13,6 +16,7 @@
 NEGATIVE = -1e30
 BF = jnp.bfloat16
 F32 = jnp.float32
+MESH = pl.DeviceIdType.MESH
 
 
 def angles(places):
@@ -52,7 +56,1090 @@
     return lax.dot_general(a, b, (((0,), (0,)), ((), ())), preferred_element_type=F32)
 
 
+def plane():
+    f = lax.axis_index("fsdp")
+    core, x, y = f % 2, (f // 2) % 2, f // 4
+    by_x, by_y = f + 2 - 4 * x, f + 4 - 8 * y
+    twin = f + 1 - 2 * core
+    near = by_x + core * (by_y - by_x)
+    far = by_y + core * (by_x - by_y)
+    return twin, near, far, 2 + 2 * core, 4 - 2 * core
+
+
+def tiles(rows, step, body):
+    count = rows // step
+    unroll = count if count <= 10 else 4
+
+    @pl.loop(0, count, unroll=unroll)
+    def _(r):
+        body(pl.ds(pl.multiple_of(r * step, step), step))
+
+
+def peer(r):
+    f = lax.axis_index("fsdp")
+    core, x, y = f % 2, (f // 2) % 2, f // 4
+    return f + (r % 2) * (1 - 2 * core) + ((r // 2) % 2) * (2 - 4 * x) + (r // 4) * (4 - 8 * y)
+
+
+def greet(others):
+    barrier = pltpu.get_barrier_semaphore()
+    for other in others:
+        pl.semaphore_signal(barrier, inc=1, device_id=other, device_id_type=MESH)
+    pl.semaphore_wait(barrier, len(others))
+
+
+def push(src, dst, send, recv, other):
+    return pltpu.make_async_remote_copy(
+        src_ref=src, dst_ref=dst, send_sem=send, recv_sem=recv, device_id=other, device_id_type=MESH
+    )
+
+
+class Gather:
+    def __init__(self, place, mine, full, send, recv, by_owner=False):
+        self.twin, self.near, self.far, self.s_near, self.s_far = place
+        self.mine, self.full, self.send, self.recv = mine, full, send, recv
+        self.by_owner = by_owner
+
+    def copy(self, i):
+        twin, near, far = self.twin, self.near, self.far
+        here = (0, 0, 0, self.s_near, 2, 4, 6)[i]
+        there, other = (
+            (self.s_near, near), (self.s_far, far), (1, twin), (6, far), (3, twin), (5, twin), (7, twin)
+        )[i]
+        if self.by_owner:
+            here = there = peer(here)
+        src = self.mine if i < 3 else self.full.at[here]
+        return push(src, self.full.at[there], self.send.at[i], self.recv.at[there], {"fsdp": other})
+
+    def start(self):
+        for i in range(3):
+            self.copy(i).start()
+
+    def wait(self, slot):
+        slot = peer(slot) if self.by_owner else slot
+        full = self.full.at[slot]
+        push(full, full, self.send.at[0], self.recv.at[slot], {"fsdp": self.near}).wait_recv()
+
+    def relay(self):
+        self.wait(2)
+        self.wait(4)
+        for i in range(3, 6):
+            self.copy(i).start()
+
+    def relay_corner(self):
+        self.wait(6)
+        self.copy(6).start()
+
+    def finish(self):
+        for i in range(7):
+            self.copy(i).wait_send()
+
+
+class Scatter:
+    def __init__(
+        self, place, part, core_in, tree_in, folded, send_core, recv_core, send_tree, recv_tree,
+        by_owner=False,
+    ):
+        self.twin, self.near, self.far, self.s_near, self.s_far = place
+        self.at = peer if by_owner else lambda slot: slot
+        self.part, self.core_in, self.tree_in, self.folded = part, core_in, tree_in, folded
+        self.send_core, self.recv_core = send_core, recv_core
+        self.send_tree, self.recv_tree = send_tree, recv_tree
+
+    def to_twin(self, k):
+        return push(
+            self.part.at[self.at(2 * k + 1)], self.core_in.at[k], self.send_core.at[k], self.recv_core.at[k],
+            {"fsdp": self.twin},
+        )
+
+    def tree(self, j):
+        other = (self.far, self.near, self.far)[j]
+        return push(
+            self.folded.at[j], self.tree_in.at[j], self.send_tree.at[j], self.recv_tree.at[j],
+            {"fsdp": other},
+        )
+
+    def fold(self, j, slot, corner=False):
+        part, core_in, tree_in, folded = self.part, self.core_in, self.tree_in, self.folded
+        k = slot // 2
+        slot = self.at(slot)
+
+        def add(at):
+            value = part[slot, at, :].astype(F32) + core_in[k, at, :].astype(F32)
+            if corner:
+                value = value + tree_in[0, at, :].astype(F32)
+            folded[j, at, :] = value.astype(BF)
+
+        tiles(part.shape[1], 16, add)
+
+    def start_corner(self):
+        self.to_twin(3).wait_recv()
+        self.fold(0, 6)
+        self.tree(0).start()
+
+    def start_far(self):
+        self.to_twin(1).wait_recv()
+        self.to_twin(2).wait_recv()
+        self.fold(2, self.s_far)
+        self.tree(2).start()
+
+    def start(self):
+        self.start_corner()
+        self.start_far()
+
+    def relay(self):
+        self.tree(0).wait_recv()
+        self.fold(1, self.s_near, True)
+        self.tree(1).start()
+
+    def total(self, store):
+        part, core_in, tree_in = self.part, self.core_in, self.tree_in
+        mine = self.at(0)
+        self.to_twin(0).wait_recv()
+        self.tree(1).wait_recv()
+        self.tree(2).wait_recv()
+
+        def add(at):
+            value = part[mine, at, :].astype(F32) + core_in[0, at, :].astype(F32)
+            store(at, value + tree_in[1, at, :].astype(F32) + tree_in[2, at, :].astype(F32))
+
+        tiles(part.shape[1], 16, add)
+
+    def finish(self):
+        for k in range(4):
+            self.to_twin(k).wait_send()
+        for j in range(3):
+            self.tree(j).wait_send()
+
+
+def line():
+    z = lax.axis_index("ctx")
+    inner = (z == 1) | (z == 2)
+    return z, inner, z + 1 - 2 * (z // 3), 3 * (z // 2), 3 - z
+
+
+class Line:
+    def __init__(self, own, pair, mate, sems, first=0):
+        self.own, self.pair, self.mate = own, pair, mate
+        self.sems, self.first = sems, first
+        self.z, self.inner, self.to_inner, self.to_outer, self.to_mate = line()
+
+    def _copy(self, k, p):
+        src, dst, other = (
+            (self.own, self.pair, self.to_inner),
+            (self.pair, self.mate, self.to_mate),
+            (self.pair, self.pair, self.to_outer),
+        )[k]
+        i = self.first + p
+        return push(src.at[p], dst.at[p], self.sems[2 * k].at[i], self.sems[2 * k + 1].at[i], {"ctx": other})
+
+    def _rows(self, body):
+        tiles(self.own.shape[1], 16, body)
+
+    def start(self, p):
+        @pl.when(~self.inner)
+        def _():
+            self._copy(0, p).start()
+
+    def meet(self, p):
+        own, pair = self.own, self.pair
+
+        @pl.when(self.inner)
+        def _():
+            self._copy(0, p).wait_recv()
+
+            def add(at):
+                pair[p, at, :] = (pair[p, at, :].astype(F32) + own[p, at, :].astype(F32)).astype(BF)
+
+            self._rows(add)
+            self._copy(1, p).start()
+
+    def settle(self, p):
+        pair, mate = self.pair, self.mate
+
+        @pl.when(self.inner)
+        def _():
+            self._copy(1, p).wait_recv()
+            self._copy(1, p).wait_send()
+
+            def add(at):
+                pair[p, at, :] = (pair[p, at, :].astype(F32) + mate[p, at, :].astype(F32)).astype(BF)
+
+            self._rows(add)
+            self._copy(2, p).start()
+
+        @pl.when(~self.inner)
+        def _():
+            self._copy(2, p).wait_recv()
+
+    def finish(self, p):
+        @pl.when(self.inner)
+        def _():
+            self._copy(2, p).wait_send()
+
+        @pl.when(~self.inner)
+        def _():
+            self._copy(0, p).wait_send()
+
+
+def greet_all():
+    z = lax.axis_index("ctx")
+    barrier = pltpu.get_barrier_semaphore()
+    for r in range(1, 8):
+        pl.semaphore_signal(barrier, inc=1, device_id={"fsdp": peer(r)}, device_id_type=MESH)
+
+    for d in range(1, 4):
+        pl.semaphore_signal(barrier, inc=1, device_id={"ctx": (z + d) % 4}, device_id_type=MESH)
+    pl.semaphore_wait(barrier, 10)
+
+
+class LineGather:
+    def __init__(self, full, send_up, send_down, recv):
+        self.full, self.send_up, self.send_down, self.recv = full, send_up, send_down, recv
+        self.z = lax.axis_index("ctx")
+
+    def _copy(self, slot, up):
+        send = (self.send_up if up else self.send_down).at[slot]
+        full = self.full.at[slot]
+        return push(full, full, send, self.recv.at[slot], {"ctx": self.z + 1 if up else self.z - 1})
+
+    def _hand_up(self, slot):
+        @pl.when(self.z < 3)
+        def _():
+            self._copy(slot, True).start()
+
+    def _hand_down(self, slot):
+        @pl.when(self.z > 0)
+        def _():
+            self._copy(slot, False).start()
+
+    def start(self):
+        self._hand_up(self.z)
+        self._hand_down(self.z)
+
+    def collect(self, d):
+        @pl.when(self.z >= d)
+        def _():
+            self._copy(self.z - d, True).wait_recv()
+            self._hand_up(self.z - d)
+
+        @pl.when(self.z + d <= 3)
+        def _():
+            self._copy(self.z + d, False).wait_recv()
+            self._hand_down(self.z + d)
+
+    def finish(self):
+        for slot in range(4):
+            @pl.when((self.z < 3) & (slot <= self.z))
+            def _():
+                self._copy(slot, True).wait_send()
+
+            @pl.when((self.z > 0) & (slot >= self.z))
+            def _():
+                self._copy(slot, False).wait_send()
+
+
+def turn(u, cosine, sine):
+    lane = lax.broadcasted_iota(jnp.int32, u.shape, 1)
+    other = jnp.where(lane % 64 < 32, pltpu.roll(u, 96, 1), pltpu.roll(u, 32, 1))
+    return u * cosine + other * sine
+
+
+def halves(pair, out):
+    lane = lax.broadcasted_iota(jnp.int32, pair.shape, 1)
+    left = lane < 64
+    swapped = pltpu.roll(pair, 64, 1)
+    zero = jnp.zeros_like(pair)
+    out[0, 0] = jnp.where(left, pair, zero).astype(BF)
+    out[0, 1] = jnp.where(left, swapped, zero).astype(BF)
+    out[1, 0] = jnp.where(left, zero, swapped).astype(BF)
+    out[1, 1] = jnp.where(left, zero, pair).astype(BF)
+
+
+def halves_t(pair, out, here):
+    pair = pair.T
+    zero = jnp.zeros((64, pair.shape[1]), BF)
+    for g in range(2):
+        head = pair[64 * g : 64 * g + 64].astype(BF)
+        out[0, g, :64, here] = head
+        out[0, g, 64:, here] = zero
+        out[1, g, :64, here] = zero
+        out[1, g, 64:, here] = head
+
+
+def key_places(kv_ref, kcol):
+    rows = kcol.shape[1]
+    for j in range(4):
+        digit = kv_ref[j, rows:, :].astype(F32)
+        places = jnp.broadcast_to(digit[0:1] * 32.0 + digit[1:2], (128, rows))
+        for lo in range(0, rows, 128):
+            column = places[:, lo : lo + 128].T
+            kcol[j * rows + lo : j * rows + lo + 128, :128] = column
+            kcol[j * rows + lo : j * rows + lo + 128, 128:] = column
+
+
+def scan_rows(count, body, init):
+    return lax.fori_loop(
+        0, count, lambda t, carry: body(pl.ds(pl.multiple_of(t * 64, 64), 64), carry), init, unroll=4
+    )
+
+
+def eights(value, op):
+    parts = [value[8 * j : 8 * j + 8] for j in range(value.shape[0] // 8)]
+    while len(parts) > 1:
+        parts = [op(parts[j], parts[j + 1]) for j in range(0, len(parts), 2)]
+    return parts[0]
+
+
+def front_kernel(
+    x_ref, pos_ref, cos_ref, sin_ref, wq_ref, wk_ref, wv_ref, wo_ref,
+    n1_ref, bq_ref, bk_ref, bv_ref, n2_ref, wg_ref, wu_ref, cot_ref,
+    xn_ref, q_ref, kv_ref, lse_ref, obt_ref, mid_ref, xn2_ref,
+    wkv_ref, wq_all, wo_all, vec_ref, wgu_ref, df_ref,
+    wkv_own, small_f, small_own, small_all, wgu_out, kk, vvt, score, prob, kcol, *sems,
+):
+    place = plane()
+    me = lax.axis_index("fsdp")
+    z = lax.axis_index("ctx")
+    rows = x_ref.shape[0]
+    ff_own, ff = wg_ref.shape[1] // 8, wgu_ref.shape[2] // 2
+    greet_all()
+    gkv = Gather(place, wkv_own, wkv_ref, sems[0], sems[1], by_owner=True)
+    gs = Gather(place, small_own, small_all, sems[2], sems[3], by_owner=True)
+    gq = Gather(place, wq_ref, wq_all, sems[4], sems[5], by_owner=True)
+    go = Gather(place, wo_ref, wo_all, sems[6], sems[7], by_owner=True)
+    send_u, recv_u = sems[8:10]
+    gk = LineGather(kv_ref, *sems[10:13])
+    gd = Gather(place, cot_ref, df_ref, sems[13], sems[14])
+
+    wkv_own[:, :128] = wk_ref[...]
+    wkv_own[:, 128:] = wv_ref[...]
+    gkv.start()
+    small_f[...] = jnp.zeros_like(small_f)
+    small_f[0:1, :112] = n1_ref[...].astype(F32)
+    small_f[1:2, :112] = bq_ref[...].astype(F32)
+    small_f[2:3, :16] = bk_ref[...].astype(F32)
+    small_f[2:3, 128:144] = bv_ref[...].astype(F32)
+    small_f[3:4, :112] = n2_ref[...].astype(F32)
+    flat = small_f[...]
+    row = lax.broadcasted_iota(jnp.int32, flat.shape, 0)
+    placed = jnp.where(row == 2, pltpu.roll(flat, me * 16, 1), pltpu.roll(flat, me * 112, 1))
+    small_own[...] = placed.astype(BF)
+    gs.start()
+    gq.start()
+    wkv_ref[me] = wkv_own[...]
+    small_all[me] = small_own[...]
+    wq_all[me] = wq_ref[...]
+    wo_all[me] = wo_ref[...]
+    for j in range(8):
+        for half, src in ((0, wg_ref), (1, wu_ref)):
+            block = src[:, j * ff_own : (j + 1) * ff_own]
+            wgu_out[j, :, half * ff : half * ff + ff_own] = block
+            wgu_out[j, :, half * ff + ff_own : (half + 1) * ff] = jnp.zeros(
+                (src.shape[0], ff - ff_own), BF
+            )
+    df_ref[0] = cot_ref[...]
+    place_row = pos_ref[...].astype(F32)
+    high = jnp.floor(place_row * (1.0 / 32.0))
+    kv_ref[z, rows : rows + 1, :] = high.astype(BF)
+    kv_ref[z, rows + 1 : rows + 2, :] = (place_row - 32.0 * high).astype(BF)
+    kv_ref[z, rows + 2 :, :] = jnp.zeros((14, 256), BF)
+
+    gkv.relay()
+    gs.relay()
+    gkv.relay_corner()
+    gs.relay_corner()
+    for slot in (3, 5, 7, 1):
+        gkv.wait(slot)
+        gs.wait(slot)
+    vec = small_all[0].astype(F32)
+    for j in range(1, 8):
+        vec = vec + small_all[j].astype(F32)
+    vec_ref[...] = vec
+
+    def norm_one(at):
+        h = x_ref[at, :].astype(F32)
+        scale = lax.rsqrt(jnp.mean(h * h, axis=-1, keepdims=True) + EPSILON)
+        xn_ref[at, :] = (h * scale * vec_ref[0:1, :]).astype(BF)
+
+    tiles(rows, 32, norm_one)
+    cosine, sine = cos_ref[...], sin_ref[...]
+    kv = dot(xn_ref[...], wkv_ref[...].reshape(896, 256)) + vec_ref[2:3, :256]
+    kv_ref[z, :rows, :128] = turn(kv[:, :128], cosine, sine).astype(BF)
+    kv_ref[z, :rows, 128:] = kv[:, 128:].astype(BF)
+    gk.start()
+
+    gq.relay()
+    go.start()
+
+    def block_to(r):
+        owner = peer(r)
+        return push(wgu_out.at[owner], wgu_ref.at[me], send_u.at[r], recv_u.at[r], {"fsdp": owner})
+
+    @pl.loop(1, 8)
+    def _(i):
+        block_to(8 - i).start()
+
+    wgu_ref[me] = wgu_out[me]
+    gd.start()
+    gk.collect(1)
+    gq.relay_corner()
+    for slot in (3, 5, 7, 1):
+        gq.wait(slot)
+
+    @pl.loop(0, 7)
+    def _(i):
+        at = pl.ds(pl.multiple_of(i * 128, 128), 128)
+        q = dot(xn_ref[...], wq_all[:, :, at].reshape(896, 128)) + vec_ref[1:2, at]
+        q_ref[:, at] = (turn(q, cosine, sine) * 0.125).astype(BF)
+
+    gk.collect(2)
+
+    gk.collect(3)
+    for j in range(4):
+        here = pl.ds(j * rows, rows)
+        halves(kv_ref[j, :rows, :128].astype(F32), kk.at[:, :, here])
+        halves_t(kv_ref[j, :rows, 128:].astype(F32), vvt, here)
+    key_places(kv_ref, kcol)
+    count = 4 * rows // 64
+
+    @pl.loop(0, 7)
+    def _(i):
+        lanes = pl.ds(pl.multiple_of(i * 128, 128), 128)
+        o = None
+        for half in range(2):
+            head = 2 * i + half
+            score[...] = dot_t(kk[half, head // 7], q_ref[:, lanes])
+
+            def find_top(at, top):
+                s = jnp.where(kcol[at, :] <= place_row, score[at, :], NEGATIVE)
+                score[at, :] = s
+                return jnp.maximum(top, eights(s, jnp.maximum))
+
+            top = scan_rows(count, find_top, jnp.full((8, rows), NEGATIVE, F32))
+            top = jnp.max(top, axis=0, keepdims=True)
+
+            def soft(at, total):
+                e = jnp.exp(score[at, :] - top)
+                prob[at, :] = e.astype(BF)
+                return total + eights(e, jnp.add)
+
+            total = scan_rows(count, soft, jnp.zeros((8, rows), F32))
+            total = jnp.sum(total, axis=0, keepdims=True)
+            lse_ref[pl.ds(head, 1), :] = top + jnp.log(total)
+            part = dot(vvt[half, head // 7], prob[...]) * (1.0 / total)
+            o = part if o is None else o + part
+        obt_ref[lanes, :] = o.astype(BF)
+
+        @pl.when(i == 0)
+        def _():
+            go.relay()
+
+        @pl.when(i == 5)
+        def _():
+            go.relay_corner()
+
+    for slot in (3, 5, 7, 1):
+        go.wait(slot)
+    for lo in range(0, 896, 128):
+        mid_ref[:, lo : lo + 128] = t_dot(obt_ref[...], wo_all[:, :, lo : lo + 128].reshape(896, 128))
+
+    def norm_two(at):
+        m = mid_ref[at, :] + x_ref[at, :].astype(F32)
+        mid_ref[at, :] = m
+        scale = lax.rsqrt(jnp.mean(m * m, axis=-1, keepdims=True) + EPSILON)
+        xn2_ref[at, :] = (m * scale * vec_ref[3:4, :]).astype(BF)
+
+    tiles(rows, 32, norm_two)
+
+    @pl.loop(1, 8)
+    def _(r):
+        block_to(r).wait_send()
+        push(
+            wgu_out.at[me], wgu_ref.at[peer(r)], send_u.at[r], recv_u.at[r], {"fsdp": peer(r)}
+        ).wait_recv()
+
+    gd.relay()
+    gd.relay_corner()
+    for slot in (1, 3, 5, 7):
+        gd.wait(slot)
+    for each in (gkv, gs, gq, go, gk, gd):
+        each.finish()
+
+
+def front(x, pos, cosine, sine, wq, wk, wv, wo, n1, bq, bk, bv, n2, wg, wu, cot):
+    dma = pltpu.SemaphoreType.DMA
+    vm = pl.BlockSpec(memory_space=pltpu.VMEM)
+    vmem = pltpu.VMEM
+    out = jax.ShapeDtypeStruct
+    rows, width = x.shape
+    own = wq.shape[0]
+    ff = -(-(wg.shape[1] // 8) // 128) * 128
+    tokens = 4 * rows
+    return pl.pallas_call(
+        front_kernel,
+        out_shape=(
+            out((rows, width), BF), out((rows, width), BF), out((4, rows + 16, 256), BF),
+            out((16, rows), F32), out((width, rows), BF), out((rows, width), F32),
+            out((rows, width), BF), out((8, own, 256), BF), out((8, own, width), BF),
+            out((8, own, width), BF), out((16, width), F32), out((8, own, 2 * ff), BF),
+            out((8, rows, width), BF),
+        ),
+        in_specs=[vm] * 16,
+        out_specs=(vm,) * 13,
+        scratch_shapes=[
+            vmem((own, 256), BF), vmem((16, width), F32), vmem((16, width), BF), vmem((8, 16, width), BF),
+            vmem((8, own, 2 * ff), BF), vmem((2, 2, tokens, 128), BF), vmem((2, 2, 128, tokens), BF),
+            vmem((tokens, rows), F32), vmem((tokens, rows), BF), vmem((tokens, rows), F32),
+            dma((7,)), dma((8,)), dma((7,)), dma((8,)), dma((7,)), dma((8,)), dma((7,)), dma((8,)),
+            dma((8,)), dma((8,)), dma((4,)), dma((4,)), dma((4,)), dma((7,)), dma((8,)),
+        ],
+        compiler_params=pltpu.CompilerParams(collective_id=2, has_side_effects=True),
+    )(x, pos, cosine, sine, wq, wk, wv, wo, n1, bq, bk, bv, n2, wg, wu, cot)
+
+
+def middle_kernel(
+    xn2_ref, pos_ref, cos_ref, sin_ref, kv_ref, lse_ref, vec_ref,
+    df_hbm, wgu_hbm, wd_hbm, x_hbm, cot_hbm, mid_hbm, xn_hbm, q_hbm, obt_hbm, wkv_hbm, wq_hbm, wo_hbm,
+    out_ref, gin_ref, pair_q, pair_o, pair_k, in_u, pair_d,
+    x_all, part_out, core_in, tree_in, dx, core_f, tree_f, gwgu, gwd, mate_d, pair_u, mate_u,
+    core_o, tree_o, core_q, tree_q, core_k, tree_k,
+    own_o, mate_o, own_q, mate_q, own_k, mate_k, dkv_in, *sems,
+):
+    place = plane()
+    me = lax.axis_index("fsdp")
+    z = lax.axis_index("ctx")
+    rows, width = xn2_ref.shape
+    own = width // 8
+    ff, ff_own = wgu_hbm.shape[1] // 2, wd_hbm.shape[0]
+    tokens, keys = 8 * rows, 4 * rows
+    piece = gwd.shape[1]
+    loads = sems[38]
+    greet_all()
+    line_sems = sems[18:24]
+    ld = Line(gwd, pair_d, mate_d, line_sems, 0)
+    lu = Line(gwgu, pair_u, mate_u, line_sems, 4)
+    lo = Line(own_o, pair_o, mate_o, line_sems, 12)
+    lq = Line(own_q, pair_q, mate_q, line_sems, 13)
+    lk = Line(own_k, pair_k, mate_k, line_sems, 14)
+    send_all, recv_all, send_kv, recv_kv = sems[24:28]
+
+    def feed_forward(df_ref, wgu_ref, wd, act_all, hid_all, dgu_all, dh, part, folded):
+        gx = Gather(place, xn2_ref, x_all, sems[0], sems[1])
+        rd = Scatter(place, part, core_in, tree_in, folded, *sems[2:6])
+        gx.start()
+        fetch = [
+            pltpu.make_async_copy(wgu_hbm, wgu_ref, loads.at[0]),
+            pltpu.make_async_copy(wd_hbm, wd.at[pl.ds(0, ff_own)], loads.at[1]),
+            pltpu.make_async_copy(df_hbm, df_ref, loads.at[2]),
+        ]
+        for cp in fetch:
+            cp.start()
+        x_all[0] = xn2_ref[...]
+        wd[ff_own:] = jnp.zeros((ff - ff_own, width), BF)
+        fetch[0].wait()
+        fetch[1].wait()
+        both = lambda ref, p: ref[pl.ds(2 * p, 2)].reshape(2 * rows, ref.shape[2])
+
+        @pl.loop(0, 4)
+        def _(p):
+            @pl.when(p == 1)
+            def _():
+                gx.relay()
+
+            @pl.when(p == 3)
+            def _():
+                gx.relay_corner()
+
+            gx.wait(2 * p + 1)
+            x = both(x_all, p)
+            for n in range(0, 2 * ff, 256):
+                act_all[p, :, n : n + 256] = dot(x, wgu_ref[:, n : n + 256])
+
+            def activate(at):
+                gate, up = act_all[p, at, :ff], act_all[p, at, ff:]
+                sig = 0.5 * jnp.tanh(0.5 * gate) + 0.5
+                hid_all[p, at, :] = (gate * sig * up).astype(BF)
+
+            tiles(2 * rows, 16, activate)
+            out = dot(hid_all[p], wd[...]).astype(BF)
+            part_out[pl.ds(2 * p, 2)] = out.reshape(2, rows, width)
+
+        fetch[2].wait()
+        for p in range(4):
+            gwd[p] = t_dot(
+                hid_all[:, :, p * piece : (p + 1) * piece].reshape(tokens, piece),
+                df_ref[...].reshape(tokens, width),
+            ).astype(BF)
+            ld.start(p)
+
+        @pl.loop(0, 4)
+        def _(k):
+            p = 3 - k
+            dh[...] = dot_t(both(df_ref, p), wd[...])
+
+            def activate(at):
+                gate, up, d = act_all[p, at, :ff], act_all[p, at, ff:], dh[at, :]
+                sig = 0.5 * jnp.tanh(0.5 * gate) + 0.5
+                dgu_all[p, at, :ff] = (d * up * (sig * (1.0 + gate * (1.0 - sig)))).astype(BF)
+                dgu_all[p, at, ff:] = (d * (gate * sig)).astype(BF)
+
+            tiles(2 * rows, 16, activate)
+            value = dot_t(dgu_all[p], wgu_ref[...]).astype(BF)
+            part[pl.ds(2 * p, 2)] = value.reshape(2, rows, width)
+            rd.to_twin(p).start()
+
+            @pl.when(k == 1)
+            def _():
+                rd.start_corner()
+
+            @pl.when(k == 2)
+            def _():
+                ld.meet(0)
+
+        rd.start_far()
+        ld.meet(1)
+        rd.relay()
+
+        @pl.loop(0, 2 * ff // 256)
+        def _(n):
+            at = pl.ds(pl.multiple_of(n * 256, 256), 256)
+            value = t_dot(x_all[...].reshape(tokens, width), dgu_all[:, :, at].reshape(tokens, 256))
+            gwgu[:, :, at] = value.astype(BF).reshape(8, own, 256)
+
+            @pl.when(n == 1)
+            def _():
+                ld.meet(2)
+
+            @pl.when(n == 3)
+            def _():
+                ld.settle(0)
+
+        for r in (7, 6, 5, 4):
+            lu.start(peer(r))
+
+        def store_dx(at, value):
+            dx[at, :] = value
+
+        rd.total(store_dx)
+        gx.finish()
+        rd.finish()
+
+    pl.run_scoped(
+        feed_forward,
+        pltpu.VMEM((8, rows, width), BF), pltpu.VMEM((width, 2 * ff), BF), pltpu.VMEM((ff, width), BF),
+        pltpu.VMEM((4, 2 * rows, 2 * ff), F32), pltpu.VMEM((4, 2 * rows, ff), BF),
+        pltpu.VMEM((4, 2 * rows, 2 * ff), BF), pltpu.VMEM((2 * rows, ff), F32),
+        pltpu.VMEM((8, rows, width), BF), pltpu.VMEM((3, rows, width), BF),
+    )
+
+    def attention_back(
+        x_ref, cot_ref, mid_ref, xn_ref, q_ref, obt_ref, wkv_ref, wq_ref, wo_ref,
+        dm, da, dob, kk, kkt, vv, kcol, score, dprob, prob, dscore, dk_acc, dv_acc,
+        dq, dkv_own, dkv, dxn, small, part_o, fold_o, part_q, fold_q, part_k, fold_k, fold_f,
+    ):
+        ro = Scatter(place, part_o, core_o, tree_o, fold_o, *sems[6:10], by_owner=True)
+        rq = Scatter(place, part_q, core_q, tree_q, fold_q, *sems[10:14], by_owner=True)
+        rk = Scatter(place, part_k, core_k, tree_k, fold_k, *sems[14:18], by_owner=True)
+        rf = Scatter(place, part_out, core_f, tree_f, fold_f, *sems[28:32])
+        arrays = (
+            (mid_hbm, mid_ref), (cot_hbm, cot_ref), (obt_hbm, obt_ref), (wo_hbm, wo_ref), (q_hbm, q_ref),
+            (xn_hbm, xn_ref), (wq_hbm, wq_ref), (wkv_hbm, wkv_ref), (x_hbm, x_ref),
+        )
+        fetch = [pltpu.make_async_copy(src, dst, loads.at[3 + i]) for i, (src, dst) in enumerate(arrays)]
+        for cp in fetch:
+            cp.start()
+        for k in (3, 2, 1, 0):
+            rf.to_twin(k).start()
+        ld.meet(3)
+        ld.settle(1)
+        fetch[0].wait()
+        fetch[1].wait()
+
+        small[...] = jnp.zeros_like(small)
+
+        def norm_two(at):
+            m, g = mid_ref[at, :], dx[at, :]
+            scale = lax.rsqrt(jnp.mean(m * m, axis=-1, keepdims=True) + EPSILON)
+            weighted = vec_ref[3:4, :] * g
+            inner = jnp.mean(weighted * m, axis=-1, keepdims=True)
+            d = cot_ref[at, :].astype(F32) + scale * weighted - m * (scale * scale * scale) * inner
+            dm[at, :] = d
+            da[at, :] = d.astype(BF)
+            small[3:4, :] += jnp.sum(g * m * scale, axis=0, keepdims=True)
+
+        tiles(rows, 32, norm_two)
+        for i in range(2, 9):
+            fetch[i].wait()
+
+        @pl.loop(0, 7)
+        def _(i):
+            lanes = pl.ds(pl.multiple_of(i * 128, 128), 128)
+            part_o[:, :, lanes] = dot(obt_ref[...], da[:, lanes]).astype(BF).reshape(8, own, 128)
+
+        for k in (3, 2, 1, 0):
+            ro.to_twin(k).start()
+        dob[...] = dot_t(da[...], wo_ref[...].reshape(width, width)).astype(BF)
+        for j in range(4):
+            here = pl.ds(j * rows, rows)
+            key, value = kv_ref[j, :rows, :128].astype(F32), kv_ref[j, :rows, 128:].astype(F32)
+            halves(key, kk.at[:, :, here])
+            halves(value, vv.at[:, :, here])
+            halves_t(key, kkt, here)
+        key_places(kv_ref, kcol)
+        dk_acc[...] = jnp.zeros_like(dk_acc)
+        dv_acc[...] = jnp.zeros_like(dv_acc)
+        place_row = pos_ref[...].astype(F32)
+        cosine, sine = cos_ref[...], -sin_ref[...]
+        count = keys // 64
+
+        def keep(total):
+            def store(at, value):
+                total[0, at, :] = value.astype(BF)
+
+            return store
+
+        def gather_to(r):
+            owner = peer(r)
+            return push(pair_u.at[owner], in_u.at[me], send_all.at[r], recv_all.at[me], {"fsdp": owner})
+
+        def settle_u(r):
+            lu.settle(peer(r))
+            gather_to(r).start()
+
+        ld.settle(2)
+
+        @pl.loop(0, 7)
+        def _(i):
+            lanes = pl.ds(pl.multiple_of(i * 128, 128), 128)
+            grad = None
+            for half in range(2):
+                head = 2 * i + half
+                g = head // 7
+                score[...] = dot_t(kk[half, g], q_ref[:, lanes])
+                dprob[...] = dot_t(vv[half, g], dob[:, lanes])
+                lse_row = lse_ref[pl.ds(head, 1), :]
+
+                def find_delta(at, total):
+                    s = jnp.where(kcol[at, :] <= place_row, score[at, :], NEGATIVE)
+                    p = jnp.exp(s - lse_row)
+                    score[at, :] = p
+                    prob[at, :] = p.astype(BF)
+                    return total + eights(p * dprob[at, :], jnp.add)
+
+                delta = scan_rows(count, find_delta, jnp.zeros((8, rows), F32))
+                delta = jnp.sum(delta, axis=0, keepdims=True)
+
+                def find_score(at):
+                    dscore[at, :] = (score[at, :] * (dprob[at, :] - delta)).astype(BF)
+
+                tiles(keys, 64, find_score)
+                dv_acc[half, g] += dot(prob[...], dob[:, lanes])
+                dk_acc[half, g] += dot(dscore[...], q_ref[:, lanes])
+                term = dot(kkt[half, g], dscore[...])
+                grad = term if grad is None else grad + term
+            dq[:, lanes] = turn(grad.T * 0.125, cosine, sine).astype(BF)
+
+            @pl.when(i == 0)
+            def _():
+                ro.start()
+                rf.start()
+                lu.meet(peer(7))
+
+            @pl.when(i == 1)
+            def _():
+                ld.settle(3)
+
+            @pl.when(i == 2)
+            def _():
+                lu.meet(peer(6))
+
+            @pl.when(i == 3)
+            def _():
+                ro.relay()
+                rf.relay()
+                settle_u(7)
+
+            @pl.when(i == 4)
+            def _():
+                lu.meet(peer(5))
+
+            @pl.when(i == 5)
+            def _():
+                settle_u(6)
+                ro.total(keep(own_o))
+
+            @pl.when(i == 6)
+            def _():
+                lu.meet(peer(4))
+
+        lane = lax.broadcasted_iota(jnp.int32, (64, 128), 1)
+
+        def join(acc, at):
+            first = jnp.where(lane < 64, acc[0, 0, at, :], acc[1, 1, at, :])
+            second = jnp.where(lane < 64, acc[0, 1, at, :], acc[1, 0, at, :])
+            return first + pltpu.roll(second, 64, 1)
+
+        @pl.loop(0, 4)
+        def _(j):
+            for first in range(0, rows, 64):
+                at = pl.ds(pl.multiple_of(j * rows + first, 64), 64)
+                dkv_own[j, first : first + 64, :128] = join(dk_acc, at).astype(BF)
+                dkv_own[j, first : first + 64, 128:] = join(dv_acc, at).astype(BF)
+
+        def kv_to(d):
+            other = (z + d) % 4
+            return push(
+                dkv_own.at[other], dkv_in.at[d - 1], send_kv.at[d - 1], recv_kv.at[d - 1], {"ctx": other}
+            )
+
+        for d in (2, 1, 3):
+            kv_to(d).start()
+
+        @pl.loop(4, 8)
+        def _(i):
+            lu.start(peer(7 - i))
+
+        lo.start(0)
+        settle_u(5)
+
+        def weight_grads(grads, part, n):
+            for at in range(0, n, 128):
+                value = t_dot(xn_ref[...], grads[:, at : at + 128]).astype(BF)
+                part[:, :, at : at + 128] = value.reshape(8, own, 128)
+
+        weight_grads(dq, part_q, width)
+        for k in (3, 2, 1, 0):
+            rq.to_twin(k).start()
+        for at in range(0, width, 128):
+            wq_rows = wq_ref[...].reshape(width, width)
+            dxn[:, at : at + 128] = dot_t(dq[...], wq_rows[at : at + 128])
+        rq.start()
+        settle_u(4)
+
+        def store_out(at, value):
+            out_ref[at, :] = value + mid_ref[at, :]
+
+        rf.total(store_out)
+        for d in (1, 3, 2):
+            kv_to(d).wait_recv()
+
+        def sum_kv(at):
+            value = dkv_own[z, at, :].astype(F32)
+            for d in range(3):
+                value = value + dkv_in[d, at, :].astype(F32)
+            dkv[at, :128] = turn(value[:, :128], cos_ref[at, :], -sin_ref[at, :]).astype(BF)
+            dkv[at, 128:] = value[:, 128:].astype(BF)
+
+        tiles(rows, 32, sum_kv)
+        weight_grads(dkv, part_k, 256)
+        for at in range(0, width, 128):
+            wkv_rows = wkv_ref[...].reshape(width, 256)
+            dxn[:, at : at + 128] += dot_t(dkv[...], wkv_rows[at : at + 128])
+
+        def norm_one(at):
+            h, g = x_ref[at, :].astype(F32), dxn[at, :]
+            scale = lax.rsqrt(jnp.mean(h * h, axis=-1, keepdims=True) + EPSILON)
+            weighted = vec_ref[0:1, :] * g
+            inner = jnp.mean(weighted * h, axis=-1, keepdims=True)
+            gin_ref[at, :] = dm[at, :] + scale * weighted - h * (scale * scale * scale) * inner
+            small[0:1, :] += jnp.sum(g * h * scale, axis=0, keepdims=True)
+            small[1:2, :] += jnp.sum(dq[at, :].astype(F32), axis=0, keepdims=True)
+            small[2:3, :256] += jnp.sum(dkv[at, :].astype(F32), axis=0, keepdims=True)
+
+        tiles(rows, 32, norm_one)
+        flat = small[...]
+        line_of = lax.broadcasted_iota(jnp.int32, (16, 128), 0)
+        for j in range(8):
+            by_row = pltpu.roll(flat, (width - 112 * j) % width, 1)[:, :128]
+            by_head = pltpu.roll(flat, (width - 16 * j) % width, 1)
+            value = jnp.where(line_of == 2, by_head[:, :128], by_row)
+            lifted = pltpu.roll(by_head[:, 128:256], 2, 0)
+            value = jnp.where(line_of == 4, lifted, value)
+            part_k[j, :16, 256:] = value.astype(BF)
+            part_k[j, 16:, 256:] = jnp.zeros((own - 16, 128), BF)
+
+        for k in (3, 2, 1, 0):
+            rk.to_twin(k).start()
+        lu.meet(peer(3))
+        rk.start()
+        rq.relay()
+        lu.meet(peer(2))
+        settle_u(3)
+        rk.relay()
+        rq.total(keep(own_q))
+        lq.start(0)
+        lu.meet(peer(1))
+        rk.total(keep(own_k))
+        lk.start(0)
+        settle_u(2)
+        lu.meet(me)
+        settle_u(1)
+        lo.meet(0)
+        lu.settle(me)
+        keep_own = pltpu.make_async_copy(pair_u.at[me], in_u.at[me], loads.at[12])
+        keep_own.start()
+        lq.meet(0)
+        lo.settle(0)
+        lk.meet(0)
+        lq.settle(0)
+        lk.settle(0)
+        keep_own.wait()
+
+        @pl.loop(1, 8)
+        def _(r):
+            other = peer(r)
+            push(
+                pair_u.at[me], in_u.at[other], send_all.at[r], recv_all.at[other], {"fsdp": other}
+            ).wait_recv()
+            gather_to(r).wait_send()
+
+        for d in (1, 2, 3):
+            kv_to(d).wait_send()
+        for each in (ro, rq, rk, rf):
+            each.finish()
+
+    v = pltpu.VMEM
+    pl.run_scoped(
+        attention_back,
+        v((rows, width), BF), v((rows, width), BF), v((rows, width), F32), v((rows, width), BF),
+        v((rows, width), BF), v((width, rows), BF), v((8, own, 256), BF), v((8, own, width), BF),
+        v((8, own, width), BF),
+        v((rows, width), F32), v((rows, width), BF), v((rows, width), BF),
+        v((2, 2, keys, 128), BF), v((2, 2, 128, keys), BF), v((2, 2, keys, 128), BF),
+        v((keys, rows), F32), v((keys, rows), F32), v((keys, rows), F32),
+        v((keys, rows), BF), v((keys, rows), BF),
+        v((2, 2, keys, 128), F32), v((2, 2, keys, 128), F32),
+        v((rows, width), BF), v((4, rows, 256), BF), v((rows, 256), BF), v((rows, width), F32),
+        v((16, width), F32),
+        v((8, own, width), BF), v((3, own, width), BF), v((8, own, width), BF), v((3, own, width), BF),
+        v((8, own, 384), BF), v((3, own, 384), BF), v((3, rows, width), BF),
+    )
+
+    @pl.loop(0, 4)
+    def _(p):
+        ld.finish(p)
+
+    @pl.loop(0, 8)
+    def _(p):
+        lu.finish(p)
+
+    for each in (lo, lq, lk):
+        each.finish(0)
+
+
+def middle(xn2, pos, cosine, sine, kv, lse, vec, df_all, wgu, wd, x, cot, mid, xn, q, obt, wkv, wq, wo):
+    dma = pltpu.SemaphoreType.DMA
+    vm = pl.BlockSpec(memory_space=pltpu.VMEM)
+    hbm = pl.BlockSpec(memory_space=pl.ANY)
+    v = pltpu.VMEM
+    out = jax.ShapeDtypeStruct
+    rows, width = x.shape
+    own = width // 8
+    ff = wgu.shape[1] // 2
+    gu, gd = (8, own, 2 * ff), (4, ff // 4, width)
+    wide, narrow = (1, own, width), (1, own, 384)
+    tree = [dma((4,)), dma((4,)), dma((3,)), dma((3,))]
+    return pl.pallas_call(
+        middle_kernel,
+        out_shape=(
+            out((rows, width), F32), out((rows, width), F32), out(wide, BF), out(wide, BF), out(narrow, BF),
+            out(gu, BF), out(gd, BF),
+        ),
+        in_specs=[vm] * 7 + [hbm] * 12,
+        out_specs=(vm, vm, vm, vm, vm, hbm, vm),
+        scratch_shapes=[
+            v((8, rows, width), BF), v((8, rows, width), BF), v((4, rows, width), BF), v((3, rows, width), BF),
+            v((rows, width), F32), v((4, rows, width), BF), v((3, rows, width), BF),
+            v(gu, BF), v(gd, BF), v(gd, BF), v(gu, BF), v(gu, BF),
+            v((4, own, width), BF), v((3, own, width), BF), v((4, own, width), BF), v((3, own, width), BF),
+            v((4, own, 384), BF), v((3, own, 384), BF),
+            v(wide, BF), v(wide, BF), v(wide, BF), v(wide, BF), v(narrow, BF), v(narrow, BF),
+            v((3, rows, 256), BF),
+            dma((7,)), dma((8,)), *tree, *tree, *tree, *tree,
+            *[dma((15,))] * 6,
+            dma((8,)), dma((8,)), dma((3,)), dma((3,)), *tree,
+            *[dma((1,))] * 6, dma((13,)),
+        ],
+        compiler_params=pltpu.CompilerParams(
+            collective_id=0, has_side_effects=True, vmem_limit_bytes=67043328
+        ),
+    )(xn2, pos, cosine, sine, kv, lse, vec, df_all, wgu, wd, x, cot, mid, xn, q, obt, wkv, wq, wo)
+
+
+def results_kernel(
+    out_ref, gin_ref, tq_ref, to_ref, tk_ref, tu_ref, td_ref,
+    o_ref, i_ref, n1_ref, q_ref, bq_ref, k_ref, bk_ref, v_ref, bv_ref, w_ref, n2_ref, g_ref, u_ref, d_ref,
+):
+    o_ref[...] = out_ref[...]
+    i_ref[...] = gin_ref[...]
+    q_ref[...] = tq_ref[0].astype(F32)
+    w_ref[...] = to_ref[0].astype(F32)
+    k_ref[...] = tk_ref[0, :, :128].astype(F32)
+    v_ref[...] = tk_ref[0, :, 128:256].astype(F32)
+    small = tk_ref[0, :16, 256:].astype(F32)
+    for i, ref in enumerate((n1_ref, bq_ref, bk_ref, n2_ref, bv_ref)):
+        ref[...] = small[i : i + 1, : ref.shape[1]]
+    ff_own, ff = d_ref.shape[0], tu_ref.shape[2] // 2
+    for j in range(8):
+        def place_block(at):
+            g_ref[at, j * ff_own : (j + 1) * ff_own] = tu_ref[j, at, :ff_own].astype(F32)
+            u_ref[at, j * ff_own : (j + 1) * ff_own] = tu_ref[j, at, ff : ff + ff_own].astype(F32)
+
+        tiles(tu_ref.shape[1], 16, place_block)
+    rows = td_ref.shape[1]
+    for p in range(4):
+        count = min(rows, ff_own - p * rows)
+        d_ref[p * rows : p * rows + count] = td_ref[p, :count].astype(F32)
+
+
+def results(out, gin, tq, to, tk, tu, td, ff_own):
+    vm = pl.BlockSpec(memory_space=pltpu.VMEM)
+    rows, width = out.shape
+    own = width // 8
+    shapes = (
+        (rows, width), (rows, width), (1, own), (own, 896), (1, own), (own, 128), (1, 16), (own, 128), (1, 16),
+        (own, 896), (1, own), (own, 8 * ff_own), (own, 8 * ff_own), (ff_own, width),
+    )
+    return pl.pallas_call(
+        results_kernel,
+        out_shape=tuple(jax.ShapeDtypeStruct(shape, F32) for shape in shapes),
+        in_specs=[vm] * 7,
+        out_specs=(vm,) * 14,
+    )(out, gin, tq, to, tk, tu, td)
+
+
 def shards(
+    inputs, positions, cotangent, norm_one, w_query, b_query, key_projection, b_key,
+    value_projection, value_bias, w_out, norm_two, w_gate, w_up, w_down,
+):
+    places = positions[0]
+    turned = angles_of(places)
+    cosine, sine = jnp.cos(turned), jnp.sin(turned)
+    sine = jnp.where(jnp.arange(128)[None, :] % 64 < 32, -sine, sine)
+    own = w_query.shape[1]
+    ff_own = w_down.shape[1]
+    ff = -(-ff_own // 128) * 128
+    x, cot = inputs[0], cotangent[0]
+    xn, q, kv, lse, obt, mid, xn2, wkv, wq, wo, vec, wgu, df_all = front(
+        x, positions, cosine, sine, w_query[0], key_projection[0], value_projection[0], w_out[0],
+        norm_one, b_query, b_key, value_bias, norm_two, w_gate[0], w_up[0], cot,
+    )
+    totals = middle(
+        xn2, positions, cosine, sine, kv, lse, vec, df_all, wgu.reshape(-1, 2 * ff), w_down[0],
+        x, cot, mid, xn, q, obt, wkv, wq, wo,
+    )
+    matrix = lambda i: i in (0, 1, 3, 5, 7, 9, 11, 12, 13)
+    return tuple(g[None] if matrix(i) else g for i, g in enumerate(results(*totals, ff_own)))
+
+
+def angles_of(places):
+    half = HEAD_SIZE // 2
+    inverse = jnp.exp(jnp.arange(half, dtype=F32) * (-2.0 * math.log(ROPE_BASE) / HEAD_SIZE))
+    return places.astype(F32)[:, None] * jnp.concatenate([inverse] * 4)[None, :]
+
+
+def shards_general(
     inputs, positions, cotangent, norm_one, w_query, b_query, key_projection, b_key,
     value_projection, value_bias, w_out, norm_two, w_gate, w_up, w_down,
 ):
@@ -196,8 +1283,9 @@
 
 def solution(mesh):
     tok, row, vec = P("fsdp", "ctx", None), P(None, "fsdp", None), P(None, "fsdp")
+    fast = mesh.shape["ctx"] == 4 and mesh.shape["fsdp"] == 8
     return jax.shard_map(
-        shards,
+        shards if fast else shards_general,
         mesh=mesh,
         in_specs=(
             tok, P("fsdp", "ctx"), tok, vec, row, vec, row, vec, row, vec, row, vec, row, row, row,

time: 597 us -> 253 us (0.42); the launches traced: 588 us -> 253 us
  waiting for transfers between devices: 294 us -> 0 us
  Pallas kernels: 0 us -> 250 us
  matrix products: 109 us -> 0 us
  blocking collectives: 85.6 us -> 0 us
  other arithmetic: 36.6 us -> 2.03 us
  local copies, waits for them, and re-layouts: 29.9 us -> 0 us
  starting transfers between devices: 16.4 us -> 0 us
  between operations: 15.9 us -> 0.67 us
    pallas_call x0 -> x3, Pallas kernels: none -> 250 us  [the longest x1 162 us: middle(): pl.pallas_call(middle_kernel, out_shape=(out((rows, width), F32), out((ro...]
    reduce_scatter x4 -> x0, waiting for transfers between devices: 114 us -> none  [the longest x1 50.6 us: shards(): lax.psum_scatter(out_part, 'fsdp', scatter_dimension=0, tiled=True)]
    dot_general x21 -> x0, matrix products: 109 us -> none  [the longest x5 26.4 us: dot(): return jnp.dot(a, b, preferred_element_type=F32)]
    psum x1 -> x0, waiting for transfers between devices: 91.5 us -> none  [shards(): lax.psum((g_attn, back[0], back[1], g_down.astype(BF)), 'ctx')]
    all_gather x3 -> x0, waiting for transfers between devices: 48.9 us -> none  [the longest x1 25 us: shards(): df_all = lax.all_gather(grad_branch, 'fsdp', axis=0, tiled=True)]
    psum x1 -> x0, blocking collectives: 42.5 us -> none  [shards(): pieces = lax.psum(pieces, ('ctx', 'fsdp'))]
    all_to_all x4 -> x0, waiting for transfers between devices: 39.1 us -> none  [the longest x2 23.9 us: shards(): lax.all_to_all(g.astype(BF), 'fsdp', split_axis=0, concat_axis=1, tiled=T...]
    all_gather x2 -> x0, blocking collectives: 27.5 us -> none  [the longest x1 16 us: shards(): kv = lax.all_gather(kv, 'ctx', axis=0, tiled=True)]
  transfers between devices with their start and end apart: 12 -> 0, of which waited for: 10 -> 0; matrix products, arithmetic and copies ran while one was open for 12% -> 0% of each run, Pallas kernels for 0% -> 0%
where the time goes in v2:
time: 253 us
  Pallas kernels  250 us (99%)
    pallas_call x1, Pallas kernels, middle(): pl.pallas_call(middle_kernel, out_shape=(out((rows, width), F32), out((ro...  162 us
    pallas_call x1, Pallas kernels, front(): pl.pallas_call(front_kernel, out_shape=(out((rows, width), BF), out((rows...  80.7 us
    pallas_call x1, Pallas kernels, results(): pl.pallas_call(results_kernel, out_shape=tuple((jax.ShapeDtypeStruct(shap...  6.77 us

profile of v2, /device:TPU:0, one launch (start us, length us, event | category | flops | bytes accessed | tf_op | source)
XLA Modules:
  0.0 252.6 jit_solution(2942414459624390836)
XLA Ops:
  0.7 0.1 pad_maximum_fusion
  0.7 0.7 convert_element_type.10
  1.4 1.2 negate_select_fusion
  2.7 80.7 %shard_map.254 = (bf16[256,896]{1,0:T(8,128)(2,1)}, bf16[256,896]{1,0:T(8,128)(2,1)}, bf16[4,272,256]{2,1,0:T(8,128)(2,1)}, f32[16,256]{1,0:T(8,128)}, bf16[896,...) custom-call(bf16[256,896]{1,0:T(8,128)(2,1)} %bitcast.21, ...), custom_call_target="tpu_custom_call" | custom-call | tf_op jit(solution)/shard_map/pallas_call | solution.py:579
  83.4 162.5 %shard_map.255 = (f32[256,896]{1,0:T(8,128)}, f32[256,896]{1,0:T(8,128)}, bf16[1,112,896]{2,1,0:T(8,128)(2,1)}, bf16[1,112,896]{2,1,0:T(8,128)(2,1)}, bf16[1,112...) custom-call(bf16[256,896]{1,0:T(8,128)(2,1)} %get-tuple-element.48.xn2_ref, ...), custom_call_target="tpu_custom_call" | custom-call | tf_op jit(solution)/shard_map/pallas_call | solution.py:1043
  245.9 6.8 %shard_map.256 = (f32[256,896]{1,0:T(8,128)}, f32[256,896]{1,0:T(8,128)}, f32[1,112]{1,0:T(1,128)}, f32[112,896]{1,0:T(8,128)}, f32[1,112]{1,0:T(1,128)}, /*inde...) custom-call(f32[256,896]{1,0:T(8,128)} %get-tuple-element.61.out_ref, ...), custom_call_target="tpu_custom_call" | custom-call | tf_op jit(solution)/shard_map/pallas_call | solution.py:1104
  (2 shorter events, 0.0 us)

commit v3 on v2

--- a/solution.py
+++ b/solution.py
@@ -472,9 +472,27 @@
     gq.relay()
     go.start()
 
+    mate = z + 1 - 2 * (z % 2)
+    half_of = lambda k: pl.ds(pl.multiple_of(k * ff, 128), ff)
+    taken, given = half_of(z % 2), half_of(1 - z % 2)
+    send_z, recv_z = sems[15:17]
+
     def block_to(r):
         owner = peer(r)
-        return push(wgu_out.at[owner], wgu_ref.at[me], send_u.at[r], recv_u.at[r], {"fsdp": owner})
+        src, dst = wgu_out.at[owner, :, taken], wgu_ref.at[me, :, taken]
+        return push(src, dst, send_u.at[r], recv_u.at[r], {"fsdp": owner})
+
+    def block_from(r):
+        src, dst = wgu_out.at[me, :, taken], wgu_ref.at[peer(r), :, taken]
+        return push(src, dst, send_u.at[r], recv_u.at[r], {"fsdp": peer(r)})
+
+    def hand_over(r):
+        block = wgu_ref.at[peer(r), :, taken]
+        return push(block, block, send_z.at[r], recv_z.at[r], {"ctx": mate})
+
+    def handed(r):
+        block = wgu_ref.at[peer(r), :, given]
+        return push(block, block, send_z.at[r], recv_z.at[r], {"ctx": mate})
 
     @pl.loop(1, 8)
     def _(i):
@@ -506,30 +524,41 @@
     @pl.loop(0, 7)
     def _(i):
         lanes = pl.ds(pl.multiple_of(i * 128, 128), 128)
+        heads = (2 * i, 2 * i + 1)
+        for half in range(2):
+            score[half] = dot_t(kk[half, heads[half] // 7], q_ref[:, lanes])
+
+        def find_top(at, tops):
+            seen = kcol[at, :] <= place_row
+            found = []
+            for half in range(2):
+                s = jnp.where(seen, score[half, at, :], NEGATIVE)
+                score[half, at, :] = s
+                found.append(jnp.maximum(tops[half], eights(s, jnp.maximum)))
+            return tuple(found)
+
+        start = jnp.full((8, rows), NEGATIVE, F32)
+        tops = [jnp.max(top, axis=0, keepdims=True) for top in scan_rows(count, find_top, (start, start))]
+
+        def soft(at, totals):
+            found = []
+            for half in range(2):
+                e = jnp.exp(score[half, at, :] - tops[half])
+                prob[half, at, :] = e.astype(BF)
+                found.append(totals[half] + eights(e, jnp.add))
+            return tuple(found)
+
+        start = jnp.zeros((8, rows), F32)
+        totals = [jnp.sum(total, axis=0, keepdims=True) for total in scan_rows(count, soft, (start, start))]
         o = None
         for half in range(2):
-            head = 2 * i + half
-            score[...] = dot_t(kk[half, head // 7], q_ref[:, lanes])
-
-            def find_top(at, top):
-                s = jnp.where(kcol[at, :] <= place_row, score[at, :], NEGATIVE)
-                score[at, :] = s
-                return jnp.maximum(top, eights(s, jnp.maximum))
-
-            top = scan_rows(count, find_top, jnp.full((8, rows), NEGATIVE, F32))
-            top = jnp.max(top, axis=0, keepdims=True)
-
-            def soft(at, total):
-                e = jnp.exp(score[at, :] - top)
-                prob[at, :] = e.astype(BF)
-                return total + eights(e, jnp.add)
-
-            total = scan_rows(count, soft, jnp.zeros((8, rows), F32))
-            total = jnp.sum(total, axis=0, keepdims=True)
-            lse_ref[pl.ds(head, 1), :] = top + jnp.log(total)
-            part = dot(vvt[half, head // 7], prob[...]) * (1.0 / total)
+            lse_ref[pl.ds(heads[half], 1), :] = tops[half] + jnp.log(totals[half])
+            part = dot(vvt[half, heads[half] // 7], prob[half]) * (1.0 / totals[half])
             o = part if o is None else o + part
         obt_ref[lanes, :] = o.astype(BF)
+
+        block_from(7 - i).wait_recv()
+        hand_over(7 - i).start()
 
         @pl.when(i == 0)
         def _():
@@ -538,6 +567,11 @@
         @pl.when(i == 5)
         def _():
             go.relay_corner()
+            gd.relay()
+
+        @pl.when(i == 6)
+        def _():
+            gd.relay_corner()
 
     for slot in (3, 5, 7, 1):
         go.wait(slot)
@@ -555,12 +589,9 @@
     @pl.loop(1, 8)
     def _(r):
         block_to(r).wait_send()
-        push(
-            wgu_out.at[me], wgu_ref.at[peer(r)], send_u.at[r], recv_u.at[r], {"fsdp": peer(r)}
-        ).wait_recv()
-
-    gd.relay()
-    gd.relay_corner()
+        hand_over(r).wait_send()
+        handed(r).wait_recv()
+
     for slot in (1, 3, 5, 7):
         gd.wait(slot)
     for each in (gkv, gs, gq, go, gk, gd):
@@ -590,9 +621,9 @@
         scratch_shapes=[
             vmem((own, 256), BF), vmem((16, width), F32), vmem((16, width), BF), vmem((8, 16, width), BF),
             vmem((8, own, 2 * ff), BF), vmem((2, 2, tokens, 128), BF), vmem((2, 2, 128, tokens), BF),
-            vmem((tokens, rows), F32), vmem((tokens, rows), BF), vmem((tokens, rows), F32),
+            vmem((2, tokens, rows), F32), vmem((2, tokens, rows), BF), vmem((tokens, rows), F32),
             dma((7,)), dma((8,)), dma((7,)), dma((8,)), dma((7,)), dma((8,)), dma((7,)), dma((8,)),
-            dma((8,)), dma((8,)), dma((4,)), dma((4,)), dma((4,)), dma((7,)), dma((8,)),
+            dma((8,)), dma((8,)), dma((4,)), dma((4,)), dma((4,)), dma((7,)), dma((8,)), dma((8,)), dma((8,)),
         ],
         compiler_params=pltpu.CompilerParams(collective_id=2, has_side_effects=True),
     )(x, pos, cosine, sine, wq, wk, wv, wo, n1, bq, bk, bv, n2, wg, wu, cot)

time: 253 us -> 237 us (0.937)
  Pallas kernels: 250 us -> 234 us
    pallas_call x1, Pallas kernels: 80.7 us -> 65.2 us  [front(): pl.pallas_call(front_kernel, out_shape=(out((rows, width), BF), out((rows...]
where the time goes in v3:
time: 237 us
  Pallas kernels  234 us (99%)
    pallas_call x1, Pallas kernels, middle(): pl.pallas_call(middle_kernel, out_shape=(out((rows, width), F32), out((ro...  162 us
    pallas_call x1, Pallas kernels, front(): pl.pallas_call(front_kernel, out_shape=(out((rows, width), BF), out((rows...  65.2 us
    pallas_call x1, Pallas kernels, results(): pl.pallas_call(results_kernel, out_shape=tuple((jax.ShapeDtypeStruct(shap...  6.77 us

profile of v3, /device:TPU:0, one launch (start us, length us, event | category | flops | bytes accessed | tf_op | source)
XLA Modules:
  0.0 237.2 jit_solution(16957783651376386242)
XLA Ops:
  0.7 0.1 pad_maximum_fusion
  0.7 0.7 convert_element_type.10
  1.4 1.2 negate_select_fusion
  2.7 65.2 %shard_map.254 = (bf16[256,896]{1,0:T(8,128)(2,1)}, bf16[256,896]{1,0:T(8,128)(2,1)}, bf16[4,272,256]{2,1,0:T(8,128)(2,1)}, f32[16,256]{1,0:T(8,128)}, bf16[896,...) custom-call(bf16[256,896]{1,0:T(8,128)(2,1)} %bitcast.21, ...), custom_call_target="tpu_custom_call" | custom-call | tf_op jit(solution)/shard_map/pallas_call | solution.py:610
  67.9 162.5 %shard_map.255 = (f32[256,896]{1,0:T(8,128)}, f32[256,896]{1,0:T(8,128)}, bf16[1,112,896]{2,1,0:T(8,128)(2,1)}, bf16[1,112,896]{2,1,0:T(8,128)(2,1)}, bf16[1,112...) custom-call(bf16[256,896]{1,0:T(8,128)(2,1)} %get-tuple-element.48.xn2_ref, ...), custom_call_target="tpu_custom_call" | custom-call | tf_op jit(solution)/shard_map/pallas_call | solution.py:1074
  230.4 6.8 %shard_map.256 = (f32[256,896]{1,0:T(8,128)}, f32[256,896]{1,0:T(8,128)}, f32[1,112]{1,0:T(1,128)}, f32[112,896]{1,0:T(8,128)}, f32[1,112]{1,0:T(1,128)}, /*inde...) custom-call(f32[256,896]{1,0:T(8,128)} %get-tuple-element.61.out_ref, ...), custom_call_target="tpu_custom_call" | custom-call | tf_op jit(solution)/shard_map/pallas_call | solution.py:1135
  (2 shorter events, 0.0 us)

commit v4 on v3

--- a/solution.py
+++ b/solution.py
@@ -746,7 +746,7 @@
             def _():
                 ld.settle(0)
 
-        for r in (7, 6, 5, 4):
+        for r in (7, 6, 5):
             lu.start(peer(r))
 
         def store_dx(at, value):
@@ -900,10 +900,6 @@
                 settle_u(6)
                 ro.total(keep(own_o))
 
-            @pl.when(i == 6)
-            def _():
-                lu.meet(peer(4))
-
         lane = lax.broadcasted_iota(jnp.int32, (64, 128), 1)
 
         def join(acc, at):
@@ -927,7 +923,7 @@
         for d in (2, 1, 3):
             kv_to(d).start()
 
-        @pl.loop(4, 8)
+        @pl.loop(3, 8)
         def _(i):
             lu.start(peer(7 - i))
 
@@ -946,7 +942,6 @@
             wq_rows = wq_ref[...].reshape(width, width)
             dxn[:, at : at + 128] = dot_t(dq[...], wq_rows[at : at + 128])
         rq.start()
-        settle_u(4)
 
         def store_out(at, value):
             out_ref[at, :] = value + mid_ref[at, :]
@@ -992,17 +987,19 @@
 
         for k in (3, 2, 1, 0):
             rk.to_twin(k).start()
-        lu.meet(peer(3))
+        lu.meet(peer(4))
         rk.start()
         rq.relay()
-        lu.meet(peer(2))
-        settle_u(3)
+        lu.meet(peer(3))
+        settle_u(4)
         rk.relay()
         rq.total(keep(own_q))
         lq.start(0)
-        lu.meet(peer(1))
+        lu.meet(peer(2))
+        settle_u(3)
         rk.total(keep(own_k))
         lk.start(0)
+        lu.meet(peer(1))
         settle_u(2)
         lu.meet(me)
         settle_u(1)

time: 237 us -> 243 us (1.025)
  Pallas kernels: 234 us -> 240 us
    pallas_call x1, Pallas kernels: 162 us -> 168 us  [middle(): pl.pallas_call(middle_kernel, out_shape=(out((rows, width), F32), out((ro...]
where the time goes in v4:
time: 243 us
  Pallas kernels  240 us (99%)
    pallas_call x1, Pallas kernels, middle(): pl.pallas_call(middle_kernel, out_shape=(out((rows, width), F32), out((ro...  168 us
    pallas_call x1, Pallas kernels, front(): pl.pallas_call(front_kernel, out_shape=(out((rows, width), BF), out((rows...  65.2 us
    pallas_call x1, Pallas kernels, results(): pl.pallas_call(results_kernel, out_shape=tuple((jax.ShapeDtypeStruct(shap...  6.77 us

profile of v4, /device:TPU:0, one launch (start us, length us, event | category | flops | bytes accessed | tf_op | source)
XLA Modules:
  0.0 243.1 jit_solution(1089642467045633667)
XLA Ops:
  0.7 0.1 pad_maximum_fusion
  0.7 0.7 convert_element_type.10
  1.4 1.2 negate_select_fusion
  2.7 65.2 %shard_map.254 = (bf16[256,896]{1,0:T(8,128)(2,1)}, bf16[256,896]{1,0:T(8,128)(2,1)}, bf16[4,272,256]{2,1,0:T(8,128)(2,1)}, f32[16,256]{1,0:T(8,128)}, bf16[896,...) custom-call(bf16[256,896]{1,0:T(8,128)(2,1)} %bitcast.21, ...), custom_call_target="tpu_custom_call" | custom-call | tf_op jit(solution)/shard_map/pallas_call | solution.py:610
  67.9 168.4 %shard_map.255 = (f32[256,896]{1,0:T(8,128)}, f32[256,896]{1,0:T(8,128)}, bf16[1,112,896]{2,1,0:T(8,128)(2,1)}, bf16[1,112,896]{2,1,0:T(8,128)(2,1)}, bf16[1,112...) custom-call(bf16[256,896]{1,0:T(8,128)(2,1)} %get-tuple-element.48.xn2_ref, ...), custom_call_target="tpu_custom_call" | custom-call | tf_op jit(solution)/shard_map/pallas_call | solution.py:1071
  236.3 6.8 %shard_map.256 = (f32[256,896]{1,0:T(8,128)}, f32[256,896]{1,0:T(8,128)}, f32[1,112]{1,0:T(1,128)}, f32[112,896]{1,0:T(8,128)}, f32[1,112]{1,0:T(1,128)}, /*inde...) custom-call(f32[256,896]{1,0:T(8,128)} %get-tuple-element.61.out_ref, ...), custom_call_target="tpu_custom_call" | custom-call | tf_op jit(solution)/shard_map/pallas_call | solution.py:1132
  (2 shorter events, 0.0 us)

commit v5 on v3

--- a/solution.py
+++ b/solution.py
@@ -875,29 +875,25 @@
             def _():
                 ro.start()
                 rf.start()
-                lu.meet(peer(7))
 
             @pl.when(i == 1)
             def _():
-                ld.settle(3)
+                lu.meet(peer(7))
 
             @pl.when(i == 2)
             def _():
-                lu.meet(peer(6))
+                ld.settle(3)
 
             @pl.when(i == 3)
             def _():
                 ro.relay()
                 rf.relay()
-                settle_u(7)
-
-            @pl.when(i == 4)
+                lu.meet(peer(6))
+
+            @pl.when(i == 5)
             def _():
                 lu.meet(peer(5))
-
-            @pl.when(i == 5)
-            def _():
-                settle_u(6)
+                settle_u(7)
                 ro.total(keep(own_o))
 
             @pl.when(i == 6)
@@ -932,6 +928,7 @@
             lu.start(peer(7 - i))
 
         lo.start(0)
+        settle_u(6)
         settle_u(5)
 
         def weight_grads(grads, part, n):

time: 237 us -> 236 us (level)
  no operation moved by 1% of the time
where the time goes in v5:
time: 236 us
  Pallas kernels  233 us (99%)
    pallas_call x1, Pallas kernels, middle(): pl.pallas_call(middle_kernel, out_shape=(out((rows, width), F32), out((ro...  161 us
    pallas_call x1, Pallas kernels, front(): pl.pallas_call(front_kernel, out_shape=(out((rows, width), BF), out((rows...  65.2 us
    pallas_call x1, Pallas kernels, results(): pl.pallas_call(results_kernel, out_shape=tuple((jax.ShapeDtypeStruct(shap...  6.77 us

profile of v5, /device:TPU:0, one launch (start us, length us, event | category | flops | bytes accessed | tf_op | source)
XLA Modules:
  0.0 236.0 jit_solution(6920255654237318041)
XLA Ops:
  0.7 0.1 pad_maximum_fusion
  0.7 0.7 convert_element_type.10
  1.4 1.2 negate_select_fusion
  2.7 65.2 %shard_map.254 = (bf16[256,896]{1,0:T(8,128)(2,1)}, bf16[256,896]{1,0:T(8,128)(2,1)}, bf16[4,272,256]{2,1,0:T(8,128)(2,1)}, f32[16,256]{1,0:T(8,128)}, bf16[896,...) custom-call(bf16[256,896]{1,0:T(8,128)(2,1)} %bitcast.21, ...), custom_call_target="tpu_custom_call" | custom-call | tf_op jit(solution)/shard_map/pallas_call | solution.py:610
  67.9 161.3 %shard_map.255 = (f32[256,896]{1,0:T(8,128)}, f32[256,896]{1,0:T(8,128)}, bf16[1,112,896]{2,1,0:T(8,128)(2,1)}, bf16[1,112,896]{2,1,0:T(8,128)(2,1)}, bf16[1,112...) custom-call(bf16[256,896]{1,0:T(8,128)(2,1)} %get-tuple-element.48.xn2_ref, ...), custom_call_target="tpu_custom_call" | custom-call | tf_op jit(solution)/shard_map/pallas_call | solution.py:1071
  229.2 6.8 %shard_map.256 = (f32[256,896]{1,0:T(8,128)}, f32[256,896]{1,0:T(8,128)}, f32[1,112]{1,0:T(1,128)}, f32[112,896]{1,0:T(8,128)}, f32[1,112]{1,0:T(1,128)}, /*inde...) custom-call(f32[256,896]{1,0:T(8,128)} %get-tuple-element.61.out_ref, ...), custom_call_target="tpu_custom_call" | custom-call | tf_op jit(solution)/shard_map/pallas_call | solution.py:1132
  (2 shorter events, 0.0 us)

commit v6 on v5

--- a/solution.py
+++ b/solution.py
@@ -783,7 +783,6 @@
         for k in (3, 2, 1, 0):
             rf.to_twin(k).start()
         ld.meet(3)
-        ld.settle(1)
         fetch[0].wait()
         fetch[1].wait()
 
@@ -838,7 +837,7 @@
             lu.settle(peer(r))
             gather_to(r).start()
 
-        ld.settle(2)
+        ld.settle(1)
 
         @pl.loop(0, 7)
         def _(i):
@@ -875,6 +874,7 @@
             def _():
                 ro.start()
                 rf.start()
+                ld.settle(2)
 
             @pl.when(i == 1)
             def _():

time: 236 us -> 238 us (level)
  no operation moved by 1% of the time
where the time goes in v6:
time: 238 us; the launch traced here: 237 us
  Pallas kernels  235 us (99%)
    pallas_call x1, Pallas kernels, middle(): pl.pallas_call(middle_kernel, out_shape=(out((rows, width), F32), out((ro...  163 us
    pallas_call x1, Pallas kernels, front(): pl.pallas_call(front_kernel, out_shape=(out((rows, width), BF), out((rows...  65.2 us
    pallas_call x1, Pallas kernels, results(): pl.pallas_call(results_kernel, out_shape=tuple((jax.ShapeDtypeStruct(shap...  6.77 us

profile of v6, /device:TPU:0, one launch (start us, length us, event | category | flops | bytes accessed | tf_op | source)
XLA Modules:
  0.0 237.4 jit_solution(16137011649277498097)
XLA Ops:
  0.7 0.1 pad_maximum_fusion
  0.7 0.7 convert_element_type.10
  1.4 1.2 negate_select_fusion
  2.7 65.2 %shard_map.254 = (bf16[256,896]{1,0:T(8,128)(2,1)}, bf16[256,896]{1,0:T(8,128)(2,1)}, bf16[4,272,256]{2,1,0:T(8,128)(2,1)}, f32[16,256]{1,0:T(8,128)}, bf16[896,...) custom-call(bf16[256,896]{1,0:T(8,128)(2,1)} %bitcast.21, ...), custom_call_target="tpu_custom_call" | custom-call | tf_op jit(solution)/shard_map/pallas_call | solution.py:610
  67.9 162.7 %shard_map.255 = (f32[256,896]{1,0:T(8,128)}, f32[256,896]{1,0:T(8,128)}, bf16[1,112,896]{2,1,0:T(8,128)(2,1)}, bf16[1,112,896]{2,1,0:T(8,128)(2,1)}, bf16[1,112...) custom-call(bf16[256,896]{1,0:T(8,128)(2,1)} %get-tuple-element.48.xn2_ref, ...), custom_call_target="tpu_custom_call" | custom-call | tf_op jit(solution)/shard_map/pallas_call | solution.py:1071
  230.6 6.8 %shard_map.256 = (f32[256,896]{1,0:T(8,128)}, f32[256,896]{1,0:T(8,128)}, f32[1,112]{1,0:T(1,128)}, f32[112,896]{1,0:T(8,128)}, f32[1,112]{1,0:T(1,128)}, /*inde...) custom-call(f32[256,896]{1,0:T(8,128)} %get-tuple-element.61.out_ref, ...), custom_call_target="tpu_custom_call" | custom-call | tf_op jit(solution)/shard_map/pallas_call | solution.py:1132
  (2 shorter events, 0.0 us)
